TPU v7x, 256 devices: a whole 4x4x8 slice. The times are simulated.
256 devices in a mesh: dir: 2 (over x_hi), slab: 64 (over y, x_lo, z), tile: 2 (over core).
Axes of the slice: x: 4 (x_hi: 2, x_lo: 2; x = x_hi * 2 + x_lo), y: 4, z: 8, core: 2. Of those that a mesh axis runs over, the one named last changes fastest.
Arguments:
- voxels: float32 [4, 512, 64, 512], P(None, 'slab', 'tile'), may hold values from -2.5 to 2.5
- offsets: int32 [2, 64, 512], P('dir', 'tile'), may hold values from 0 to 511
- heading: int32 [2, 64, 512], P('dir', 'tile'), may hold values from 0 to 1
- cotangent: float32 [2, 3, 64, 512], P('dir', None, 'tile'), may hold values from -6 to 6
Outputs:
- image: float32 [2, 3, 64, 512], P('dir', None, 'tile', 'slab')
- voxel_grad: float32 [4, 512, 64, 512], P(None, 'slab', 'tile', 'dir')
Inputs may be any that keep to these rules, and one draw needn't show every extreme that they name: `offsets`: A code packs three sub-cell positions as p + 8 * m + 8 * 8 * n (p along depth, m along rows, n along columns).
All inputs are finite; a program needn't handle non-finite values.
Results may differ from a plain program's by a relative error of at most 0.0003.
Values sent between devices are 32-bit elements; how exact they have to be, the bound alone decides.
A program may use at most 64 MiB of HBM per device.

v0:
```python
import jax
import jax.numpy as jnp
from jax import lax
from jax.sharding import Mesh
from jax.sharding import PartitionSpec as P

LEVELS = 8
SLAB = ("slab_0", "slab_1", "slab_2")


def padded(block, sides, width):
    for axis, dim in sides:
        count = lax.axis_size(axis)
        forward = [(i, i + 1) for i in range(count - 1)]
        backward = [(target, source) for source, target in forward]
        low = lax.ppermute(
            lax.slice_in_dim(block, block.shape[dim] - width, None, axis=dim), axis, forward
        )
        high = lax.ppermute(lax.slice_in_dim(block, 0, width, axis=dim), axis, backward)
        block = jnp.concatenate([low, block, high], axis=dim)
    return block


def filled_with(array, identity):
    return jnp.zeros_like(array) + jnp.asarray(identity, array.dtype)


def prefix_by_axis(array, axes, combine, identity, reverse):
    before = start = filled_with(array, identity)
    subtotal = array
    for axis in reversed(axes):
        devices, position = (lax.axis_size(axis), lax.axis_index(axis))
        pieces = lax.all_gather(subtotal, axis)
        inside, subtotal = (start, start)
        for k in reversed(range(devices)) if reverse else range(devices):
            passed = k > position if reverse else k < position
            subtotal = combine(subtotal, pieces[k])
            inside = jnp.where(passed, subtotal, inside)
        before = combine(inside, before)
    return before


def in_blocks(array, dim, devices):
    lengths = array.shape
    blocks = array.reshape(*lengths[:dim], devices, lengths[dim] // devices, *lengths[dim + 1 :])
    return jnp.moveaxis(blocks, dim, 0)


def sent_and_summed(array, axis, dim):
    blocks = in_blocks(array, dim, lax.axis_size(axis))
    arrived = lax.all_to_all(blocks, axis, split_axis=0, concat_axis=0, tiled=True)
    return arrived.sum(axis=0)


def tap_weights(codes):
    level = LEVELS
    fz = (codes % level).astype(jnp.float32)
    fy = (codes // level % level).astype(jnp.float32)
    fx = (codes // (level * level)).astype(jnp.float32)

    def three(raw):
        f = (raw + 0.5) / level - 0.5
        return (jnp.maximum(-f, 0.0), 1.0 - jnp.abs(f), jnp.maximum(f, 0.0))

    return (three(fz), three(fy), three(fx))


def combine_sum(earlier, later):
    return earlier + later


def per_device(voxels, offsets, heading, cotangent):
    planes, rows, total_cols = (voxels.shape[1], voxels.shape[2], voxels.shape[3])
    depth = planes * lax.axis_size(SLAB)
    scale = 2.0 / depth
    padded_grid = padded(voxels, ((SLAB, 1), ("tile", 2)), 1)
    padded_grid = jnp.pad(padded_grid, ((0, 0), (0, 0), (0, 0), (2, 2)))
    grid = padded_grid[:, :, :, 1 : total_cols + 3]
    forward = heading == 0
    wz, wy, wx = tap_weights(offsets)
    plane = None
    for b in range(3):
        for e in range(3):
            term = (wy[b] * wx[e])[:, None, None] * grid[
                None, :, :, b : b + rows, e : e + total_cols
            ]
            plane = term if plane is None else plane + term
    values = None
    for a in range(3):
        term = wz[a][:, None, None] * plane[:, :, a : a + planes]
        values = term if values is None else values + term
    sigma = jax.nn.softplus(values[:, 0]) * scale
    colour = jax.nn.sigmoid(values[:, 1:])
    alpha = 1.0 - jnp.exp(-sigma)
    ahead = jnp.cumsum(sigma, axis=1) - sigma
    depth_sum = jnp.sum(sigma, axis=1)
    local_front = jnp.where(forward[:, None], ahead, depth_sum[:, None] - ahead - sigma)
    glow = jnp.exp(-local_front) * alpha
    local_image = jnp.sum(glow[:, None] * colour, axis=2)
    zeros = jnp.zeros_like(depth_sum)
    lower = prefix_by_axis(depth_sum, SLAB, combine_sum, zeros, False)
    higher = prefix_by_axis(depth_sum, SLAB, combine_sum, zeros, True)
    before = jnp.where(forward, lower, higher)
    reach = jnp.exp(-before)
    parts = reach[:, None] * local_image
    image = sent_and_summed(parts, SLAB, 3)
    pull = cotangent * depth
    shade = jnp.sum(pull[:, :, None] * colour, axis=1)
    local_pull = jnp.sum(glow * shade, axis=1)
    weighted = reach * local_pull
    lead_low = prefix_by_axis(weighted, SLAB, combine_sum, zeros, False)
    lead_high = prefix_by_axis(weighted, SLAB, combine_sum, zeros, True)
    lead = jnp.where(forward, lead_low, lead_high)
    whole = lead_low + weighted + lead_high
    through = reach[:, None] * glow
    share = through * shade
    before_share = jnp.cumsum(share, axis=1) - share
    share_sum = jnp.sum(share, axis=1)
    ahead_share = lead[:, None] + jnp.where(
        forward[:, None], before_share, share_sum[:, None] - before_share - share
    )
    behind = whole[:, None] - ahead_share - share
    d_sigma = jnp.exp(-(before[:, None] + local_front + sigma)) * shade - behind
    grad_density = d_sigma * jax.nn.sigmoid(values[:, 0]) * scale
    grad_colour = pull[:, :, None] * through[:, None] * colour * (1.0 - colour)
    sample_grad = jnp.concatenate([grad_density[:, None], grad_colour], axis=1)
    spread = padded(sample_grad, ((SLAB, 2), ("tile", 3)), 1)
    spread = jnp.pad(spread, ((0, 0), (0, 0), (0, 0), (0, 0), (1, 1)))
    codes_wide = padded(offsets, (("tile", 1),), 1)
    codes_wide = jnp.pad(codes_wide, ((0, 0), (0, 0), (1, 1)))
    vz, vy, vx = tap_weights(codes_wide)
    column = None
    for a in range(3):
        term = vz[a][:, None, None] * spread[:, :, 2 - a : 2 - a + planes]
        column = term if column is None else column + term
    grad = None
    for b in range(3):
        for e in range(3):
            first = 2 - e
            factor = (vy[b] * vx[e])[:, 2 - b : 2 - b + rows, first : first + total_cols]
            term = (
                factor[:, None, None]
                * column[:, :, :, 2 - b : 2 - b + rows, first : first + total_cols]
            )
            grad = term if grad is None else grad + term
    grad = jnp.sum(grad, axis=0)
    voxel_grad = sent_and_summed(grad, "dir", 3)
    return (image, voxel_grad)


def solution(mesh):
    finer = Mesh(
        mesh.devices.reshape(mesh.shape["dir"], 4, 2, 8, mesh.shape["tile"]),
        ("dir", "slab_0", "slab_1", "slab_2", "tile"),
    )
    return jax.shard_map(
        per_device,
        mesh=finer,
        in_specs=(
            P(None, SLAB, "tile", None),
            P("dir", "tile", None),
            P("dir", "tile", None),
            P("dir", None, "tile", None),
        ),
        out_specs=(P("dir", None, "tile", SLAB), P(None, SLAB, "tile", "dir")),
        check_vma=False,
    )
```

profile of v0, /device:TPU:1, one launch (start us, length us, event | category | flops | bytes accessed | tf_op | source)
XLA Modules:
  0.0 264.4 jit_solution(15603416194061673528)
XLA Ops:
  0.6 1.9 fusion.134
  2.5 4.4 %collective-permute-start = (f32[4,1,32,512]{3,2,1,0:T(8,128)}, f32[4,1,32,512]{3,2,1,0:T(8,128)S(1)}, u32[]{:S(2)}, u32[]{:S(2)}) collective-permute-start(f32[4,1,32,512]{3,2,1,0:T(8,128)} %get-tuple-element.27), channel_id=1, source_target_pairs={{0,2},{2,4},{4,6},{6,8},{8,10},{10,12},{12,14},{14,16},{16,18},{18... | collective-permute-start | bytes 786440 | tf_op jit(solution)/shard_map/ppermute | solution.py:16
  6.9 1.3 collective-permute-start.1
  8.9 1.3 collective-permute-start.4
  10.2 3.0 %collective-permute-start.5 = (s32[1,1,512]{2,1,0:T(1,128)S(1)}, s32[1,1,512]{2,1,0:T(1,128)S(1)}, u32[]{:S(2)}, u32[]{:S(2)}) collective-permute-start(s32[1,1,512]{2,1,0:T(1,128)S(1)} %get-tuple-element.61), channel_id=1, source_target_pairs={{1,0},{3,2},{5,4},{7,6},{9,8},{11,10},{13,12},{15,14},{17,16},{19,... | collective-permute-start | bytes 6152 | tf_op jit(solution)/shard_map/ppermute | solution.py:19
  13.3 2.8 %copy.16 = f32[4,8,32,512]{3,1,2,0:T(8,128)S(1)} copy(f32[4,8,32,512]{3,2,1,0:T(8,128)} %param.4) | data formatting | bytes 4194304 | tf_op args[0]
  16.4 1.6 multiply_bitcast_fusion.1
  19.5 1.3 collective-permute-start.2
  20.8 3.0 %collective-permute-start.3 = (f32[4,10,1,512]{3,1,2,0:T(8,128)S(1)}, f32[4,10,1,512]{3,1,2,0:T(8,128)S(1)}, u32[]{:S(2)}, u32[]{:S(2)}) collective-permute-start(f32[4,10,1,512]{3,1,2,0:T(8,128)S(1)} %get-tuple-element.21), channel_id=1, source_target_pairs={{1,0},{3,2},{5,4},{7,6},{9,8},{11,10},{13,12},{15,14},{17,16},{19,... | collective-permute-start | bytes 245768 | tf_op jit(solution)/shard_map/ppermute | solution.py:19
  23.8 1.2 negate_maximum_fusion
  25.1 4.4 %select_maximum_fusion.5 = f32[4,10,34,516]{3,1,2,0:T(8,128)S(1)} fusion(f32[4,10,1,512]{3,1,2,0:T(8,128)S(1)} %collective-permute-done.3, f32[4,10,1,512]{3,1,2,0:T(8,128)S(1)} %collective-permute-done.2, f32[4,1,32,512]{3,1,2,0:T(1,128)S(1)} %copy.17, f32[4,8,32,512]{3,1,2,0:T(8,128)S(1)} %copy.16, f32[4,1,32,512]{3,1,2,0:T(1,128)S(1)} %copy.15), kind=kLoop, calls=%fused_computation.9 | loop fusion | flops 8421120 | bytes 5592320 | tf_op jit(solution)/shard_map/concatenate | solution.py:20
  29.5 8.3 %fusion.3 = f32[1,4,10,32,512]{4,2,3,1,0:T(8,128)S(1)} fusion(f32[4,10,34,516]{3,1,2,0:T(8,128)S(1)} %select_maximum_fusion.5, f32[4,10,1,512]{3,1,2,0:T(8,128)S(1)} %collective-permute-done.3, f32[4,1,32,512]{3,1,2,0:T(1,128)S(1)} %copy.17, f32[4,8,32,512]{3,1,2,0:T(8,128)S(1)} %copy.16, f32[4,1,32,512]{3,1,2,0:T(1,128)S(1)} %copy.15, ...), kind=kLoop, calls=%fused_computation.17 | loop fusion | flops 16384000 | bytes 21725184 | tf_op jit(solution)/shard_map/add | solution.py:87
  38.4 1.4 fusion.130
  39.8 23.7 %all-gather = f32[256,512]{1,0:T(8,128)S(1)} all-gather(f32[32,512]{1,0:T(8,128)S(1)} %get-tuple-element.16), channel_id=2, replica_groups=mesh['dir'=2,'slab_0'=4,'slab_1'=2,'slab_2'=8,'tile'=2] {'slab_2'}, dimensions={0}, use_global_device_ids=true | all-gather | bytes 589824 | tf_op jit(solution)/shard_map/all_gather | solution.py:33
  63.6 3.8 %all_gather.50 = f32[2,1,32,512]{3,2,1,0:T(8,128)S(1)} all-gather(f32[1,1,32,512]{3,2,1,0:T(8,128)S(1)} %get-tuple-element.31), channel_id=1, replica_groups=mesh['dir'=2,'slab_0'=4,'slab_1'=2,'slab_2'=8,'tile'=2] {'slab_1'}, dimensions={0}, use_global_device_ids=true | all-gather | bytes 196608 | tf_op jit(solution)/shard_map/all_gather | solution.py:33
  67.4 12.2 %all_gather.51 = f32[4,1,32,512]{3,2,1,0:T(8,128)} all-gather(f32[1,1,32,512]{3,2,1,0:T(8,128)S(1)} %slice_add_fusion.15), channel_id=1, replica_groups=mesh['dir'=2,'slab_0'=4,'slab_1'=2,'slab_2'=8,'tile'=2] {'slab_0'}, dimensions={0}, use_global_device_ids=true | all-gather | bytes 327680 | tf_op jit(solution)/shard_map/all_gather | solution.py:33
  79.6 3.8 %all_gather.52 = f32[2,1,32,512]{3,2,1,0:T(8,128)S(1)} all-gather(f32[1,1,32,512]{3,2,1,0:T(8,128)S(1)} %get-tuple-element.32), channel_id=1, replica_groups=mesh['dir'=2,'slab_0'=4,'slab_1'=2,'slab_2'=8,'tile'=2] {'slab_1'}, dimensions={0}, use_global_device_ids=true | all-gather | bytes 196608 | tf_op jit(solution)/shard_map/all_gather | solution.py:33
  83.4 10.9 %all_gather.53 = f32[4,1,32,512]{3,2,1,0:T(8,128)} all-gather(f32[1,1,32,512]{3,2,1,0:T(8,128)S(1)} %slice_add_fusion.11), channel_id=1, replica_groups=mesh['dir'=2,'slab_0'=4,'slab_1'=2,'slab_2'=8,'tile'=2] {'slab_0'}, dimensions={0}, use_global_device_ids=true | all-gather | bytes 327680 | tf_op jit(solution)/shard_map/all_gather | solution.py:33
  94.3 1.5 reduce_window_sum.21
  95.8 1.3 fusion.125
  97.7 3.3 %multiply_reduce_fusion = (f32[8,32,512]{2,0,1:T(8,128)S(1)}, f32[3,32,512]{2,1,0:T(8,128)}, f32[1,3,8,32,512]{4,2,3,1,0:T(8,128)S(1)}) fusion(f32[3,32,512]{2,1,0:T(8,128)} %multiply_bitcast_fusion.1, f32[1,4,8,32,512]{4,2,3,1,0:T(8,128)} %copy-done, f32[8,32,512]{2,0,1:T(8,128)S(1)} %bitcast.387, f32[8,32,512]{2,0,1:T(8,128)S(1)} %get-tuple-element.11), kind=kLoop, calls=%fused_computation.72 | loop fusion | flops 4145152 | bytes 5111808 | tf_op jit(solution)/shard_map/reduce_sum | solution.py:108
  101.0 2.5 multiply_reduce_fusion.3
  105.1 18.9 %all-gather.1 = f32[8,32,512]{2,1,0:T(8,128)S(1)} all-gather(f32[1,32,512]{2,1,0:T(8,128)S(1)} %get-tuple-element.62), channel_id=3, replica_groups=mesh['dir'=2,'slab_0'=4,'slab_1'=2,'slab_2'=8,'tile'=2] {'slab_2'}, dimensions={0}, use_global_device_ids=true | all-gather | bytes 589824 | tf_op jit(solution)/shard_map/all_gather | solution.py:33
  124.0 3.8 %all_gather.56 = f32[2,1,32,512]{3,2,1,0:T(8,128)S(1)} all-gather(f32[1,1,32,512]{3,2,1,0:T(8,128)S(1)} %get-tuple-element.29), channel_id=1, replica_groups=mesh['dir'=2,'slab_0'=4,'slab_1'=2,'slab_2'=8,'tile'=2] {'slab_1'}, dimensions={0}, use_global_device_ids=true | all-gather | bytes 196608 | tf_op jit(solution)/shard_map/all_gather | solution.py:33
  127.8 10.4 %all_gather.57 = f32[4,1,32,512]{3,2,1,0:T(8,128)} all-gather(f32[1,1,32,512]{3,2,1,0:T(8,128)S(1)} %slice_add_fusion.7), channel_id=1, replica_groups=mesh['dir'=2,'slab_0'=4,'slab_1'=2,'slab_2'=8,'tile'=2] {'slab_0'}, dimensions={0}, use_global_device_ids=true | all-gather | bytes 327680 | tf_op jit(solution)/shard_map/all_gather | solution.py:33
  138.2 4.1 %all_gather.58 = f32[2,1,32,512]{3,2,1,0:T(8,128)S(1)} all-gather(f32[1,1,32,512]{3,2,1,0:T(8,128)S(1)} %get-tuple-element.30), channel_id=1, replica_groups=mesh['dir'=2,'slab_0'=4,'slab_1'=2,'slab_2'=8,'tile'=2] {'slab_1'}, dimensions={0}, use_global_device_ids=true | all-gather | bytes 196608 | tf_op jit(solution)/shard_map/all_gather | solution.py:33
  142.3 10.1 %all_gather.59 = f32[4,1,32,512]{3,2,1,0:T(8,128)} all-gather(f32[1,1,32,512]{3,2,1,0:T(8,128)S(1)} %slice_add_fusion.3), channel_id=1, replica_groups=mesh['dir'=2,'slab_0'=4,'slab_1'=2,'slab_2'=8,'tile'=2] {'slab_0'}, dimensions={0}, use_global_device_ids=true | all-gather | bytes 327680 | tf_op jit(solution)/shard_map/all_gather | solution.py:33
  152.4 2.3 reduce_window_sum.24
  154.7 1.4 add_bitcast_fusion
  156.1 2.1 fusion.38
  158.2 1.1 pad_maximum_fusion.8
  159.3 1.3 collective-permute-start.6
  160.6 1.3 collective-permute-start.7
  162.0 1.0 fusion.87
  163.9 1.2 copy.20
  165.2 2.9 %collective-permute-done.7 = f32[1,4,1,32,512]{4,2,3,1,0:T(1,128)} collective-permute-done((f32[1,4,1,32,512]{4,2,3,1,0:T(1,128)}, f32[1,4,1,32,512]{4,2,3,1,0:T(1,128)}, u32[]{:S(2)}, u32[]{:S(2)}) %collective-permute-start.7) | collective-permute-done | bytes 262176 | tf_op jit(solution)/shard_map/ppermute | solution.py:19
  168.0 1.5 pad_maximum_fusion.12
  169.5 1.3 collective-permute-start.8
  170.8 32.5 %collective-permute-start.9 = (f32[1,4,10,1,512]{4,2,3,1,0:T(8,128)}, f32[1,4,10,1,512]{4,2,3,1,0:T(8,128)}, u32[]{:S(2)}, u32[]{:S(2)}) collective-permute-start(f32[1,4,10,1,512]{4,2,3,1,0:T(8,128)} %get-tuple-element.23), channel_id=1, source_target_pairs={{1,0},{3,2},{5,4},{7,6},{9,8},{11,10},{13,12},{15,14},{17,16},{19,... | collective-permute-start | bytes 245768 | tf_op jit(solution)/shard_map/ppermute | solution.py:19
  204.3 2.2 reshape.1448
  206.4 13.5 %all-to-all-start = ((f32[64,1,768]{2,1,0:T(1,128)}), f32[64,1,768]{2,1,0:T(1,128)S(1)}, u32[]{:S(2)}, u32[]{:S(2)}) async-start(f32[64,1,768]{2,1,0:T(1,128)} %reshape.1448), calls=%async_computation | async-start | bytes 393216 | tf_op jit(solution)/shard_map/all_to_all | solution.py:51
  220.0 5.8 %select_maximum_fusion = f32[1,4,10,34,514]{4,2,3,1,0:T(8,128)S(1)} fusion(f32[1,4,10,1,512]{4,2,3,1,0:T(8,128)} %collective-permute-done.9, f32[1,4,10,1,512]{4,2,3,1,0:T(8,128)} %collective-permute-done.8, f32[1,4,1,32,512]{4,2,3,1,0:T(1,128)} %collective-permute-done.7, f32[1,4,1,32,512]{4,2,3,1,0:T(1,128)S(1)} %collective-permute-done.6, ...), kind=kLoop, calls=%fused_computation.4 | loop fusion | flops 9786560 | bytes 5581440 | tf_op jit(solution)/shard_map/concatenate | solution.py:20
  227.0 3.7 %fusion.15 = f32[1,4,8,32,512]{4,2,3,1,0:T(8,128)S(1)} fusion(f32[1,4,8,34,514]{4,2,3,1,0:T(8,128)S(1)} %fusion.13, f32[32,512]{1,0:T(8,128)S(1)} %copy-done.11, f32[32,512]{1,0:T(8,128)S(1)} %copy-done.13, f32[32,512]{1,0:T(8,128)S(1)} %copy-done.12, f32[32,512]{1,0:T(8,128)S(1)} %copy-done.16, f32[32,512]{1,0:T(8,128)S(1)} %copy-done.15, ...), kind=kLoop, calls=%fused_computation.45 | loop fusion | flops 8912896 | bytes 21561344 | tf_op jit(solution)/shard_map/add | solution.py:145
  230.7 2.5 copy.26
  233.2 3.8 %all-to-all-start.1 = ((f32[2,4,8,32,256]{4,3,2,1,0:T(8,128)}), f32[2,4,8,32,256]{4,3,2,1,0:T(8,128)S(1)}, u32[]{:S(2)}, u32[]{:S(2)}) async-start(f32[2,4,8,32,256]{4,3,2,1,0:T(8,128)} %bitcast.385), calls=%async_computation.1 | async-start | bytes 4194304 | tf_op jit(solution)/shard_map/all_to_all | solution.py:51
  237.5 1.1 reduce.8
  239.6 23.7 %all-to-all-done.1 = f32[2,4,8,32,256]{4,3,2,1,0:T(8,128)S(1)} async-done(((f32[2,4,8,32,256]{4,3,2,1,0:T(8,128)}), f32[2,4,8,32,256]{4,3,2,1,0:T(8,128)S(1)}, u32[]{:S(2)}, u32[]{:S(2)}) %all-to-all-start.1) | async-done | bytes 2097184 | tf_op jit(solution)/shard_map/all_to_all | solution.py:51
  263.2 1.2 reduce_sum.85
  (72 shorter events, 9.7 us)
Async XLA Ops:
  0.6 15.4 %copy-start.5 = (s32[1,32,512]{2,1,0:T(8,128)S(1)}, s32[1,32,512]{2,1,0:T(8,128)}, u32[]{:S(2)}) copy-start(s32[1,32,512]{2,1,0:T(8,128)} %param.5) | copy-start | bytes 196612
  2.5 15.5 %collective-permute-start = (f32[4,1,32,512]{3,2,1,0:T(8,128)}, f32[4,1,32,512]{3,2,1,0:T(8,128)S(1)}, u32[]{:S(2)}, u32[]{:S(2)}) collective-permute-start(f32[4,1,32,512]{3,2,1,0:T(8,128)} %get-tuple-element.27), channel_id=1, source_target_pairs={{0,2},{2,4},{4,6},{6,8},{8,10},{10,12},{12,14},{14,16},{16,18},{18... | collective-permute-start | bytes 786440 | tf_op jit(solution)/shard_map/ppermute | solution.py:16
  6.9 11.4 %collective-permute-start.1 = (f32[4,1,32,512]{3,2,1,0:T(8,128)}, f32[4,1,32,512]{3,2,1,0:T(8,128)S(1)}, u32[]{:S(2)}, u32[]{:S(2)}) collective-permute-start(f32[4,1,32,512]{3,2,1,0:T(8,128)} %get-tuple-element.28), channel_id=1, source_target_pairs={{2,0},{4,2},{6,4},{8,6},{10,8},{12,10},{14,12},{16,14},{18,16},{20... | collective-permute-start | bytes 786440 | tf_op jit(solution)/shard_map/ppermute | solution.py:19
  8.9 9.1 %collective-permute-start.4 = (s32[1,1,512]{2,1,0:T(1,128)S(1)}, s32[1,1,512]{2,1,0:T(1,128)S(1)}, u32[]{:S(2)}, u32[]{:S(2)}) collective-permute-start(s32[1,1,512]{2,1,0:T(1,128)S(1)} %get-tuple-element.60), channel_id=1, source_target_pairs={{0,1},{2,3},{4,5},{6,7},{8,9},{10,11},{12,13},{14,15},{16,17},{18,... | collective-permute-start | bytes 6152 | tf_op jit(solution)/shard_map/ppermute | solution.py:16
  10.2 7.8 %collective-permute-start.5 = (s32[1,1,512]{2,1,0:T(1,128)S(1)}, s32[1,1,512]{2,1,0:T(1,128)S(1)}, u32[]{:S(2)}, u32[]{:S(2)}) collective-permute-start(s32[1,1,512]{2,1,0:T(1,128)S(1)} %get-tuple-element.61), channel_id=1, source_target_pairs={{1,0},{3,2},{5,4},{7,6},{9,8},{11,10},{13,12},{15,14},{17,16},{19,... | collective-permute-start | bytes 6152 | tf_op jit(solution)/shard_map/ppermute | solution.py:19
  19.5 5.6 %collective-permute-start.2 = (f32[4,10,1,512]{3,1,2,0:T(8,128)S(1)}, f32[4,10,1,512]{3,1,2,0:T(8,128)S(1)}, u32[]{:S(2)}, u32[]{:S(2)}) collective-permute-start(f32[4,10,1,512]{3,1,2,0:T(8,128)S(1)} %get-tuple-element.20), channel_id=1, source_target_pairs={{0,1},{2,3},{4,5},{6,7},{8,9},{10,11},{12,13},{14,15},{16,17},{18,... | collective-permute-start | bytes 245768 | tf_op jit(solution)/shard_map/ppermute | solution.py:16
  20.8 4.3 %collective-permute-start.3 = (f32[4,10,1,512]{3,1,2,0:T(8,128)S(1)}, f32[4,10,1,512]{3,1,2,0:T(8,128)S(1)}, u32[]{:S(2)}, u32[]{:S(2)}) collective-permute-start(f32[4,10,1,512]{3,1,2,0:T(8,128)S(1)} %get-tuple-element.21), channel_id=1, source_target_pairs={{1,0},{3,2},{5,4},{7,6},{9,8},{11,10},{13,12},{15,14},{17,16},{19,... | collective-permute-start | bytes 245768 | tf_op jit(solution)/shard_map/ppermute | solution.py:19
  38.4 59.3 %copy-start = (f32[1,4,8,32,512]{4,2,3,1,0:T(8,128)}, f32[1,4,8,32,512]{4,2,3,1,0:T(8,128)S(1)}, u32[]{:S(2)}) copy-start(f32[1,4,8,32,512]{4,2,3,1,0:T(8,128)S(1)} %fusion.23) | copy-start | bytes 6291460
  105.1 18.9 %copy-start.6 = (f32[1,32,512]{2,1,0:T(8,128)}, f32[1,32,512]{2,1,0:T(8,128)S(1)}, u32[]{:S(2)}) copy-start(f32[1,32,512]{2,1,0:T(8,128)S(1)} %get-tuple-element.62) | copy-start | bytes 196612
  154.7 7.3 %copy-start.7 = (f32[1,34,514]{2,1,0:T(8,128)S(1)}, f32[1,34,514]{2,1,0:T(8,128)}, u32[]{:S(2)}) copy-start(f32[1,34,514]{2,1,0:T(8,128)} %get-tuple-element.58) | copy-start | bytes 209716
  154.7 7.3 %copy-start.1 = (f32[1,34,514]{2,1,0:T(8,128)S(1)}, f32[1,34,514]{2,1,0:T(8,128)}, u32[]{:S(2)}) copy-start(f32[1,34,514]{2,1,0:T(8,128)} %get-tuple-element.52) | copy-start | bytes 209716
  154.7 7.3 %copy-start.2 = (f32[1,34,514]{2,1,0:T(8,128)S(1)}, f32[1,34,514]{2,1,0:T(8,128)}, u32[]{:S(2)}) copy-start(f32[1,34,514]{2,1,0:T(8,128)} %get-tuple-element.55) | copy-start | bytes 209716
  154.7 7.3 %copy-start.3 = (f32[1,34,514]{2,1,0:T(8,128)S(1)}, f32[1,34,514]{2,1,0:T(8,128)}, u32[]{:S(2)}) copy-start(f32[1,34,514]{2,1,0:T(8,128)} %get-tuple-element.56) | copy-start | bytes 209716
  154.7 7.3 %copy-start.4 = (f32[1,34,514]{2,1,0:T(8,128)S(1)}, f32[1,34,514]{2,1,0:T(8,128)}, u32[]{:S(2)}) copy-start(f32[1,34,514]{2,1,0:T(8,128)} %get-tuple-element.57) | copy-start | bytes 209716
  159.3 5.8 %collective-permute-start.6 = (f32[1,4,1,32,512]{4,2,3,1,0:T(1,128)}, f32[1,4,1,32,512]{4,2,3,1,0:T(1,128)S(1)}, u32[]{:S(2)}, u32[]{:S(2)}) collective-permute-start(f32[1,4,1,32,512]{4,2,3,1,0:T(1,128)} %get-tuple-element.25), channel_id=1, source_target_pairs={{0,2},{2,4},{4,6},{6,8},{8,10},{10,12},{12,14},{14,16},{16,18},{18... | collective-permute-start | bytes 786440 | tf_op jit(solution)/shard_map/ppermute | solution.py:16
  160.6 7.4 %collective-permute-start.7 = (f32[1,4,1,32,512]{4,2,3,1,0:T(1,128)}, f32[1,4,1,32,512]{4,2,3,1,0:T(1,128)}, u32[]{:S(2)}, u32[]{:S(2)}) collective-permute-start(f32[1,4,1,32,512]{4,2,3,1,0:T(1,128)} %get-tuple-element.26), channel_id=1, source_target_pairs={{2,0},{4,2},{6,4},{8,6},{10,8},{12,10},{14,12},{16,14},{18,16},{20... | collective-permute-start | bytes 786440 | tf_op jit(solution)/shard_map/ppermute | solution.py:19
  169.5 50.5 %collective-permute-start.8 = (f32[1,4,10,1,512]{4,2,3,1,0:T(8,128)}, f32[1,4,10,1,512]{4,2,3,1,0:T(8,128)}, u32[]{:S(2)}, u32[]{:S(2)}) collective-permute-start(f32[1,4,10,1,512]{4,2,3,1,0:T(8,128)} %get-tuple-element.22), channel_id=1, source_target_pairs={{0,1},{2,3},{4,5},{6,7},{8,9},{10,11},{12,13},{14,15},{16,17},{18,... | collective-permute-start | bytes 245768 | tf_op jit(solution)/shard_map/ppermute | solution.py:16
  170.8 49.2 %collective-permute-start.9 = (f32[1,4,10,1,512]{4,2,3,1,0:T(8,128)}, f32[1,4,10,1,512]{4,2,3,1,0:T(8,128)}, u32[]{:S(2)}, u32[]{:S(2)}) collective-permute-start(f32[1,4,10,1,512]{4,2,3,1,0:T(8,128)} %get-tuple-element.23), channel_id=1, source_target_pairs={{1,0},{3,2},{5,4},{7,6},{9,8},{11,10},{13,12},{15,14},{17,16},{19,... | collective-permute-start | bytes 245768 | tf_op jit(solution)/shard_map/ppermute | solution.py:19
  206.4 26.8 %all-to-all-start = ((f32[64,1,768]{2,1,0:T(1,128)}), f32[64,1,768]{2,1,0:T(1,128)S(1)}, u32[]{:S(2)}, u32[]{:S(2)}) async-start(f32[64,1,768]{2,1,0:T(1,128)} %reshape.1448), calls=%async_computation | async-start | bytes 393216 | tf_op jit(solution)/shard_map/all_to_all | solution.py:51
  220.0 5.9 %copy-start.8 = (f32[34,514]{1,0:T(8,128)S(1)}, f32[34,514]{1,0:T(8,128)}, u32[]{:S(2)}) copy-start(f32[34,514]{1,0:T(8,128)} %get-tuple-element.53) | copy-start | bytes 209716
  220.0 5.9 %copy-start.9 = (f32[34,514]{1,0:T(8,128)S(1)}, f32[34,514]{1,0:T(8,128)}, u32[]{:S(2)}) copy-start(f32[34,514]{1,0:T(8,128)} %get-tuple-element.54) | copy-start | bytes 209716
  220.0 5.9 %copy-start.10 = (f32[34,514]{1,0:T(8,128)S(1)}, f32[34,514]{1,0:T(8,128)}, u32[]{:S(2)}) copy-start(f32[34,514]{1,0:T(8,128)} %get-tuple-element.59) | copy-start | bytes 209716
  225.9 0.9 copy-start.11
  225.9 0.9 copy-start.12
  225.9 0.9 copy-start.13
  226.0 0.9 copy-start.14
  226.0 0.9 copy-start.15
  226.0 1.0 copy-start.16
  226.0 1.0 copy-start.17
  233.2 30.0 %all-to-all-start.1 = ((f32[2,4,8,32,256]{4,3,2,1,0:T(8,128)}), f32[2,4,8,32,256]{4,3,2,1,0:T(8,128)S(1)}, u32[]{:S(2)}, u32[]{:S(2)}) async-start(f32[2,4,8,32,256]{4,3,2,1,0:T(8,128)} %bitcast.385), calls=%async_computation.1 | async-start | bytes 4194304 | tf_op jit(solution)/shard_map/all_to_all | solution.py:51
where the time goes:
time: 266 us; the launch traced here: 264 us
  blocking collectives  102 us (38%)
  starting transfers between devices  68 us (26%)
  other arithmetic  53.2 us (20%)
  waiting for transfers between devices  26.6 us (10%)
  local copies, waits for them, and re-layouts  13.8 us (5%)
    all_gather x10, blocking collectives, prefix_by_axis(): pieces = lax.all_gather(subtotal, axis)  102 us
    ppermute x5, starting transfers between devices, padded(): lax.ppermute(lax.slice_in_dim(block, 0, width, axis=dim), axis, backward)  41.2 us
    all_to_all x2, waiting for transfers between devices, sent_and_summed(): lax.all_to_all(blocks, axis, split_axis=0, concat_axis=0, tiled=True)  23.7 us
    all_to_all x2, starting transfers between devices, sent_and_summed(): lax.all_to_all(blocks, axis, split_axis=0, concat_axis=0, tiled=True)  17.3 us
    concatenate x4, other arithmetic, padded(): block = jnp.concatenate([low, block, high], axis=dim)  11.1 us
    ppermute x5, starting transfers between devices, padded(): lax.ppermute(lax.slice_in_dim(block, block.shape[dim] - width, None, axis...  9.51 us
    add x1, other arithmetic, per_device(): plane = term if plane is None else plane + term  8.28 us
    unnamed x39, local copies, waits for them, and re-layouts  5.42 us
  transfers between devices with their start and end apart: 12, of which 2 were waited for; matrix products, arithmetic and copies ran while one was open for 11% of the time, Pallas kernels for 0%

commit v1 on v0

v1 whole, which is shorter than its diff:
```python
import functools

import jax
import jax.numpy as jnp
from jax import lax
from jax.experimental import pallas as pl
from jax.experimental.pallas import tpu as pltpu
from jax.sharding import Mesh
from jax.sharding import PartitionSpec as P

LEVELS = 8
AXES = ("dir", "sy", "sx", "sz", "tile")
SLAB = ("sy", "sx", "sz")
MESH = pl.DeviceIdType.MESH
ANY = pl.BlockSpec(memory_space=pl.ANY)
VM = pl.BlockSpec(memory_space=pltpu.VMEM)


def places():
    return {a: lax.axis_index(a) for a in AXES}


def slab_index(me):
    sx, sz = lax.axis_size("sx"), lax.axis_size("sz")
    return (me["sy"] * sx + me["sx"]) * sz + me["sz"]


def at_slab(me, step):
    sy, sx, sz = (lax.axis_size(a) for a in SLAB)
    s = lax.rem(slab_index(me) + step + sy * sx * sz, sy * sx * sz)
    return dict(me, sy=s // (sx * sz), sx=(s // sz) % sx, sz=s % sz)


def ident(place):
    return tuple(place[a] for a in AXES)


def greet(peers):
    barrier = pltpu.get_barrier_semaphore()
    for peer in peers:
        pl.semaphore_signal(barrier, inc=1, device_id=ident(peer), device_id_type=MESH)
    pl.semaphore_wait(barrier, len(peers))


def push(src, dst, send, recv, peer):
    return pltpu.make_async_remote_copy(
        src_ref=src, dst_ref=dst, send_sem=send, recv_sem=recv,
        device_id=ident(peer), device_id_type=MESH,
    )


def halo_kernel(win, half, vox, codes, head, cot,
                zp, zn, rh, zpr, znr, oc, oh, oct_, send, recv):
    me = places()
    d, t = me["dir"], me["tile"]
    prev, nxt = at_slab(me, -1), at_slab(me, 1)
    flip = lambda p: dict(p, tile=1 - p["tile"])
    mate = dict(me, dir=1 - d, sx=lax.axis_size("sx") - 1 - me["sx"])
    greet([prev, nxt, flip(me), flip(prev), flip(nxt), mate])
    planes, rows = vox.shape[1], vox.shape[2]
    cols = pl.ds(pl.multiple_of(d * (half - (win - half)), win - half), win)
    edge = pl.ds(pl.multiple_of((1 - t) * (rows - 8), 8), 8)
    theirs = pl.ds(pl.multiple_of((1 - d) * half, half), half)
    jobs = [
        (vox.at[:, planes - 1, :, cols], zp, nxt),
        (vox.at[:, 0, :, cols], zn, prev),
        (codes.at[0, :, theirs], oc, mate),
        (head.at[0, :, theirs], oh, mate),
        (vox.at[:, planes - 1, edge, cols], zpr, flip(nxt)),
        (vox.at[:, 0, edge, cols], znr, flip(prev)),
        (vox.at[:, :, edge, cols], rh, flip(me)),
        (cot.at[0, :, :, theirs], oct_, mate),
    ]
    copies = [push(a, b, send.at[i], recv.at[i], p) for i, (a, b, p) in enumerate(jobs)]
    for copy in copies:
        copy.start()
    for copy in copies:
        copy.wait()


def exchange_halos(voxels, offsets, heading, cotangent):
    ch, planes, rows, total = voxels.shape
    half = total // 2
    win = half + half // 2
    f32 = lambda *s: jax.ShapeDtypeStruct(s, jnp.float32)
    i32 = lambda *s: jax.ShapeDtypeStruct(s, jnp.int32)
    return pl.pallas_call(
        functools.partial(halo_kernel, win, half),
        out_shape=(f32(ch, rows, win), f32(ch, rows, win), f32(ch, planes, 8, win),
                   f32(ch, 8, win), f32(ch, 8, win),
                   i32(rows, half), i32(rows, half), f32(3, rows, half)),
        in_specs=[ANY] * 4,
        out_specs=(ANY,) * 8,
        scratch_shapes=[pltpu.SemaphoreType.DMA((8,)), pltpu.SemaphoreType.DMA((8,))],
        compiler_params=pltpu.CompilerParams(collective_id=0, has_side_effects=True),
    )(voxels, offsets, heading, cotangent)


def scan_kernel(dl, im, hd, rb, img, rdl, rim, gm, ret, part, rpart,
                s1, r1, s2, r2, s3, r3, s4, r4, s5, r5):
    me = places()
    nsy, nsx, nz = (lax.axis_size(a) for a in SLAB)
    ng = nsy * nsx
    blocks = ng // 2
    z = me["sz"]
    gi = me["sy"] * nsx + me["sx"]
    d = me["dir"]
    lanes = dl.shape[-1]
    rows = lanes // 4

    zpeer = [dict(me, sz=lax.rem(z + i, nz)) for i in range(1, nz)]
    gpeer = []
    for i in range(1, ng):
        g = lax.rem(gi + i, ng)
        gpeer.append(dict(me, sy=g // nsx, sx=g % nsx))
    across = []
    for i in range(ng):
        g = lax.rem(gi + i, ng)
        across.append(dict(me, dir=1 - d, sy=g // nsx, sx=g % nsx))
    greet(zpeer + gpeer + across)

    first = [push(dl.at[p["sz"]], rdl.at[z], s1.at[i], r1.at[i], p) for i, p in enumerate(zpeer)]
    for c in first:
        c.start()
    late = [push(im.at[p["sz"]], rim.at[z], s2.at[i], r2.at[i], p) for i, p in enumerate(zpeer)]
    for c in late:
        c.start()
    rdl[z] = dl[z]
    rim[z] = im[z]
    ahead = hd[z] == 0
    lane = lax.broadcasted_iota(jnp.int32, ahead.shape, 2)
    is_d = (lane // rows) % 2 == 0
    for c in first:
        c.wait()
    roll = lambda a, n: pltpu.roll(a, n % lanes, 2)

    def directed(parts):
        lows, total = [], jnp.zeros_like(parts[0])
        for p in parts:
            lows.append(total)
            total = total + p
        highs, back = [], jnp.zeros_like(parts[0])
        for p in reversed(parts):
            highs.append(back)
            back = back + p
        highs = highs[::-1]
        before = [jnp.where(ahead, a, b) for a, b in zip(lows, highs)]
        after = [jnp.where(ahead, b, a) for a, b in zip(lows, highs)]
        return before, after, total

    tiles = [rdl[i] for i in range(nz)]
    before, _, dsum = directed(tiles)
    reach = [jnp.exp(-b) for b in before]
    pulled = [roll(r, rows) * t for r, t in zip(reach, tiles)]
    _, behind, lsum = directed(pulled)
    gm[gi] = jnp.where(is_d, dsum, lsum)
    second = [push(gm.at[gi], gm.at[gi], s3.at[i], r3.at[i], p) for i, p in enumerate(gpeer)]
    for c in second:
        c.start()
    for c in second:
        c.wait()
    groups = [gm[i] for i in range(ng)]
    gbefore, _, _ = directed(groups)
    greach = [jnp.exp(-b) for b in gbefore]
    gpull = [roll(r, rows) * t for r, t in zip(greach, groups)]
    _, gafter, _ = directed(gpull)
    mine = jnp.zeros_like(dsum)
    rest = jnp.zeros_like(dsum)
    for i in range(ng):
        mine = jnp.where(gi == i, greach[i], mine)
        rest = jnp.where(gi == i, gafter[i], rest)
    mine_l = roll(mine, rows)
    full = []
    for i in range(nz):
        r = mine * reach[i]
        full.append(r)
        ret[i] = jnp.where(is_d, r, rest + mine_l * behind[i])
    back = [push(ret.at[p["sz"]], rb.at[z], s4.at[i], r4.at[i], p) for i, p in enumerate(zpeer)]
    for c in back:
        c.start()
    rb[z] = ret[z]
    for c in late:
        c.wait()
    quarter = lane // rows
    for b in range(2):
        total = jnp.zeros_like(dsum)
        for i in range(nz):
            src = full[i]
            spread = roll(src, -2 * b * rows)
            spread = jnp.where(quarter == 1, roll(src, (1 - 2 * b) * rows), spread)
            spread = jnp.where(quarter == 2, roll(src, (2 - 2 * b) * rows), spread)
            total = total + spread * rim[i, b]
        part[b] = total
    half_of_me = gi // blocks
    out = []
    for b in range(2):
        for m in range(blocks):
            g = blocks * d + m
            peer = dict(me, dir=d if b == 0 else 1 - d, sy=g // nsx, sx=g % nsx)
            out.append(push(part.at[b, m], rpart.at[gi], s5.at[b * blocks + m], r5.at[gi], peer))
    for b in range(2):
        for m in range(blocks):
            copy = out[b * blocks + m]
            if b == 0:
                itself = gi == blocks * d + m

                @pl.when(itself)
                def _():
                    rpart[gi] = part[0, m]

                @pl.when(jnp.logical_not(itself))
                def _():
                    copy.start()
            else:
                copy.start()
    for b in range(2):
        for m in range(blocks):
            copy = out[b * blocks + m]
            if b == 0:
                @pl.when(gi != blocks * d + m)
                def _():
                    copy.wait_send()
            else:
                copy.wait_send()
    for i in range(ng):
        arrive = push(part.at[0, 0], rpart.at[i], s5.at[0], r5.at[i], dict(me, dir=1 - d))

        @pl.when(jnp.logical_or(half_of_me != d, gi != i))
        def _():
            arrive.wait_recv()
    total = rpart[0]
    for i in range(1, ng):
        total = total + rpart[i]
    img[...] = total
    for c in back:
        c.wait()


def scan_slabs(dl, im, hd):
    nz, m, c8, lanes = dl.shape
    nsy, nsx = lax.axis_size("sy"), lax.axis_size("sx")
    ng = nsy * nsx
    f32 = lambda *s: pltpu.VMEM(s, jnp.float32)
    dma = pltpu.SemaphoreType.DMA
    return pl.pallas_call(
        scan_kernel,
        out_shape=(jax.ShapeDtypeStruct(dl.shape, jnp.float32),
                   jax.ShapeDtypeStruct((c8, lanes), jnp.float32)),
        in_specs=[VM] * 3,
        out_specs=(VM, VM),
        scratch_shapes=[
            f32(*dl.shape), f32(*im.shape), f32(ng, m, c8, lanes), f32(*dl.shape),
            f32(2, m, c8, lanes), f32(ng, c8, lanes),
            dma((nz - 1,)), dma((nz - 1,)), dma((nz - 1,)), dma((nz - 1,)),
            dma((ng - 1,)), dma((ng - 1,)), dma((nz - 1,)), dma((nz - 1,)),
            dma((ng,)), dma((ng,)),
        ],
        compiler_params=pltpu.CompilerParams(collective_id=1, has_side_effects=True),
    )(dl, im, hd)


def spill_kernel(zup, zdn, line, pack, fp, fn, rline, rpack, send, recv):
    me = places()
    prev, nxt = at_slab(me, -1), at_slab(me, 1)
    flip = lambda p: dict(p, tile=1 - p["tile"])
    over = lambda p: dict(p, dir=1 - p["dir"])
    near = [prev, me, nxt]
    greet([prev, nxt] + [flip(p) for p in near] + [over(p) for p in near]
          + [over(flip(p)) for p in near])
    jobs = [(zup, fp, nxt), (zdn, fn, prev)]
    for i, p in enumerate(near):
        jobs.append((line, rline.at[2 - i], flip(p)))
    for i, p in enumerate(near):
        jobs.append((pack, rpack.at[2 - i, 0], over(p)))
        jobs.append((pack, rpack.at[2 - i, 1], over(flip(p))))
    copies = [push(a, b, send.at[i], recv.at[i], p) for i, (a, b, p) in enumerate(jobs)]
    for copy in copies:
        copy.start()
    for copy in copies:
        copy.wait()


def exchange_spill(zup, zdn, line, pack):
    s = jax.ShapeDtypeStruct
    return pl.pallas_call(
        spill_kernel,
        out_shape=(s(zup.shape, jnp.float32), s(zdn.shape, jnp.float32),
                   s((3,) + line.shape, jnp.float32), s((3, 2) + pack.shape, jnp.float32)),
        in_specs=[VM] * 4,
        out_specs=(VM,) * 4,
        scratch_shapes=[pltpu.SemaphoreType.DMA((11,)), pltpu.SemaphoreType.DMA((11,))],
        compiler_params=pltpu.CompilerParams(collective_id=2, has_side_effects=True),
    )(zup, zdn, line, pack)


def tap_weights(codes):
    level = LEVELS
    fz = (codes % level).astype(jnp.float32)
    fy = (codes // level % level).astype(jnp.float32)
    fx = (codes // (level * level)).astype(jnp.float32)

    def three(raw):
        f = (raw + 0.5) / level - 0.5
        return (jnp.maximum(-f, 0.0), 1.0 - jnp.abs(f), jnp.maximum(f, 0.0))

    return (three(fz), three(fy), three(fx))


def to_tiles(stacked, nz):
    lanes, cols = stacked.shape
    tiles = stacked.T.reshape(cols // 8 // nz, nz, 8, lanes)
    return jnp.moveaxis(tiles, 1, 0)


def from_tiles(tiles):
    nz, m, c8, lanes = tiles.shape
    return jnp.moveaxis(tiles, 0, 1).reshape(m * nz * c8, lanes).T


def per_device(voxels, offsets, heading, cotangent):
    ch, planes, rows, total = voxels.shape
    nz = lax.axis_size("sz")
    slabs = lax.axis_size(SLAB)
    depth = planes * slabs
    scale = 2.0 / depth
    half = total // 2
    ext = half // 2
    win = half + ext
    me = places()
    d, t, s = me["dir"], me["tile"], slab_index(me)
    zp, zn, rh, zpr, znr, oc, oh, oct_ = exchange_halos(voxels, offsets, heading, cotangent)

    own = lambda a: lax.dynamic_slice_in_dim(a[0], d * half, half, axis=a.ndim - 2)
    codes = jnp.stack([own(offsets), oc])
    head = jnp.stack([own(heading), oh])
    pull = jnp.stack([own(cotangent), oct_]) * depth
    forward = head == 0

    zp = jnp.where(s > 0, zp, 0.0)
    zpr = jnp.where(s > 0, zpr, 0.0)
    zn = jnp.where(s < slabs - 1, zn, 0.0)
    znr = jnp.where(s < slabs - 1, znr, 0.0)
    core = lax.dynamic_slice_in_dim(voxels, d * (half - ext), win, axis=3)
    body = jnp.concatenate([zp[:, None], core, zn[:, None]], axis=1)
    side = jnp.concatenate([zpr[:, None], rh, znr[:, None]], axis=1)
    top = jnp.where(t == 1, side[:, :, 7:8], 0.0)
    low = jnp.where(t == 0, side[:, :, 0:1], 0.0)
    grid = jnp.concatenate([top, body, low], axis=2)
    grid = jnp.pad(grid, ((0, 0), (0, 0), (0, 0), (1, 1)))
    grid = lax.dynamic_slice_in_dim(grid, d * (half - ext), half + 2, axis=3)

    wz, wy, wx = tap_weights(codes)
    plane = None
    for b in range(3):
        for e in range(3):
            term = (wy[b] * wx[e])[:, None, None] * grid[None, :, :, b:b + rows, e:e + half]
            plane = term if plane is None else plane + term
    values = None
    for a in range(3):
        term = wz[a][:, None, None] * plane[:, :, a:a + planes]
        values = term if values is None else values + term
    sigma = jax.nn.softplus(values[:, 0]) * scale
    colour = jax.nn.sigmoid(values[:, 1:])
    alpha = 1.0 - jnp.exp(-sigma)
    ahead = jnp.cumsum(sigma, axis=1) - sigma
    depth_sum = jnp.sum(sigma, axis=1)
    front = jnp.where(forward[:, None], ahead, depth_sum[:, None] - ahead - sigma)
    through = jnp.exp(-front)
    glow = through * alpha
    local_image = jnp.sum(glow[:, None] * colour, axis=2)
    shade = jnp.sum(pull[:, :, None] * colour, axis=1)
    local_pull = jnp.sum(pull * local_image, axis=1)

    stacked = jnp.stack([depth_sum, local_pull], axis=1).reshape(4 * rows, half)
    dl = to_tiles(stacked, nz)
    blank = jnp.zeros_like(depth_sum)[:, None]
    images = jnp.concatenate([local_image, blank], axis=1).reshape(2, 4 * rows, half)
    im = jnp.stack([to_tiles(images[0], nz), to_tiles(images[1], nz)], axis=1)
    hd = to_tiles(jnp.stack([head, head], axis=1).reshape(4 * rows, half), nz)
    rb, img = scan_slabs(dl, im, hd)
    image = img.T.reshape(4, rows, 8)[None, :3]
    rb = from_tiles(rb).reshape(2, 2, rows, half)
    reach, rest = rb[:, 0], rb[:, 1]

    lit = reach[:, None] * glow
    share = lit * shade
    share_before = jnp.cumsum(share, axis=1) - share
    share_sum = jnp.sum(share, axis=1)
    behind = rest[:, None] + jnp.where(
        forward[:, None], share_sum[:, None] - share_before - share, share_before
    )
    d_sigma = reach[:, None] * (through - glow) * shade - behind
    grad_density = d_sigma * jax.nn.sigmoid(values[:, 0]) * scale
    grad_colour = pull[:, :, None] * lit[:, None] * colour * (1.0 - colour)
    grads = jnp.concatenate([grad_density[:, None], grad_colour], axis=1)

    padded = jnp.pad(grads, ((0, 0), (0, 0), (2, 2), (0, 0), (0, 0)))
    column = None
    for a in range(3):
        term = wz[a][:, None, None] * padded[:, :, 2 - a:2 - a + planes + 2]
        column = term if column is None else column + term
    wide = None
    for b in range(3):
        for e in range(3):
            term = jnp.sum((wy[b] * wx[e])[:, None, None] * column, axis=0)
            term = jnp.pad(term, ((0, 0), (0, 0), (b, 2 - b), (e, 2 - e)))
            wide = term if wide is None else wide + term
    inner = wide[:, :, 1:rows + 1, 1:half + 1]
    line = jnp.where(t == 0, wide[:, :, rows + 1], wide[:, :, 0])
    edge = jnp.where(d == 0, wide[..., half + 1], wide[..., 0])
    far = jnp.where(t == 0, edge[:, :, rows + 1], edge[:, :, 0])
    packs = ch * (planes + 2)
    pack = jnp.concatenate([edge[:, :, 1:rows + 1], far[:, :, None]], axis=2)
    pack = pack.reshape(packs, rows + 1).T
    pack = jnp.pad(pack, ((0, 7), (0, 128 - packs)))
    line = line[:, :, 1:half + 1].reshape(packs, half)

    fp, fn, rline, rpack = exchange_spill(inner[:, -1], inner[:, 0], line, pack)
    has_prev, has_next = s > 0, s < slabs - 1
    grad = inner[:, 1:-1]
    grad = grad.at[:, 0].add(jnp.where(has_prev, fp, 0.0))
    grad = grad.at[:, -1].add(jnp.where(has_next, fn, 0.0))
    rline = rline.reshape(3, ch, planes + 2, half)
    row = rline[1, :, 1:-1]
    row = row.at[:, 0].add(jnp.where(has_prev, rline[0, :, -1], 0.0))
    row = row.at[:, -1].add(jnp.where(has_next, rline[2, :, 0], 0.0))
    rpack = rpack[..., :rows + 1, :packs].reshape(3, 2, rows + 1, ch, planes + 2)
    rim = rpack[1, :, :, :, 1:-1]
    rim = rim.at[..., 0].add(jnp.where(has_prev, rpack[0, ..., -1], 0.0))
    rim = rim.at[..., -1].add(jnp.where(has_next, rpack[2, ..., 0], 0.0))
    touch = (1 - t) * (rows - 1)
    grad = jnp.where(
        lax.broadcasted_iota(jnp.int32, grad.shape, 2) == touch, grad + row[:, :, None], grad
    )
    col = rim[0, :rows]
    col = jnp.where(
        lax.broadcasted_iota(jnp.int32, col.shape, 0) == touch, col + rim[1, rows], col
    )
    col = jnp.moveaxis(col, 0, -1)
    seam = (1 - d) * (half - 1)
    grad = jnp.where(
        lax.broadcasted_iota(jnp.int32, grad.shape, 3) == seam, grad + col[..., None], grad
    )
    return (image, grad)


def solution(mesh):
    n = mesh.devices.size
    shape = (2, 4, 2, 8, 2) if n == 256 else (2, 2, 1, 2, 2)
    finer = Mesh(mesh.devices.reshape(shape), AXES)
    return jax.shard_map(
        per_device,
        mesh=finer,
        in_specs=(
            P(None, SLAB, "tile", None),
            P("dir", "tile", None),
            P("dir", "tile", None),
            P("dir", None, "tile", None),
        ),
        out_specs=(P("dir", None, "tile", SLAB), P(None, SLAB, "tile", "dir")),
        check_vma=False,
    )
```

time: 266 us -> 126 us (0.47)
  blocking collectives: 102 us -> 0 us
  starting transfers between devices: 68 us -> 0 us
  Pallas kernels: 0 us -> 56.4 us
  waiting for transfers between devices: 26.6 us -> 0 us
  local copies, waits for them, and re-layouts: 13.8 us -> 35.2 us
  other arithmetic: 53.2 us -> 32 us
    all_gather x10 -> x0, blocking collectives: 102 us -> none  [prefix_by_axis(): pieces = lax.all_gather(subtotal, axis)]
    pallas_call x0 -> x3, Pallas kernels: none -> 56.4 us  [the longest x1 19.6 us: scan_slabs(): pl.pallas_call(scan_kernel, out_shape=(jax.ShapeDtypeStruct(dl.shape, jnp...]
    ppermute x10 -> x0, starting transfers between devices: 50.7 us -> none  [the longest x5 41.2 us: padded(): lax.ppermute(lax.slice_in_dim(block, 0, width, axis=dim), axis, backward)]
    all_to_all x2 -> x0, waiting for transfers between devices: 23.7 us -> none  [sent_and_summed(): lax.all_to_all(blocks, axis, split_axis=0, concat_axis=0, tiled=True)]
    all_to_all x2 -> x0, starting transfers between devices: 17.3 us -> none  [sent_and_summed(): lax.all_to_all(blocks, axis, split_axis=0, concat_axis=0, tiled=True)]
    concatenate x4 -> x2, other arithmetic: 11.1 us -> 3.78 us  [the longest x1 3.33 us: per_device(): grid = jnp.concatenate([top, body, low], axis=2)]
    mul x9 -> x4, other arithmetic: 8.42 us -> 1.56 us  [the longest x2 0.98 us: per_device(): grad_colour = pull[:, :, None] * lit[:, None] * colour * (1.0 - colour)]
    transpose x0 -> x5, local copies, waits for them, and re-layouts: none -> 6.53 us  [the longest x2 3.32 us: to_tiles(): tiles = stacked.T.reshape(cols // 8 // nz, nz, 8, lanes)]
  transfers between devices with their start and end apart: 12 -> 0, of which waited for: 2 -> 0; matrix products, arithmetic and copies ran while one was open for 11% -> 0% of each run, Pallas kernels for 0% -> 0%
where the time goes in v1:
time: 126 us; the launch traced here: 125 us
  Pallas kernels  56.4 us (45%)
  local copies, waits for them, and re-layouts  35.2 us (28%)
  other arithmetic  32 us (25%)
  between operations  1.42 us (1%)
    pallas_call x1, Pallas kernels, scan_slabs(): pl.pallas_call(scan_kernel, out_shape=(jax.ShapeDtypeStruct(dl.shape, jnp...  19.6 us
    pallas_call x1, Pallas kernels, exchange_spill(): pl.pallas_call(spill_kernel, out_shape=(s(zup.shape, jnp.float32), s(zdn....  18.8 us
    pallas_call x1, Pallas kernels, exchange_halos(): pl.pallas_call(functools.partial(halo_kernel, win, half), out_shape=(f32(...  18 us
    slice x1, local copies, waits for them, and re-layouts, per_device(): grid[None, :, :, b:b + rows, e:e + half]  6.51 us
    reshape x4, local copies, waits for them, and re-layouts, to_tiles(): tiles = stacked.T.reshape(cols // 8 // nz, nz, 8, lanes)  5.57 us
    add x1, other arithmetic, per_device(): plane = term if plane is None else plane + term  5.44 us
    reduce_sum x1, other arithmetic, per_device(): term = jnp.sum((wy[b] * wx[e])[:, None, None] * column, axis=0)  4.3 us
    add x1, other arithmetic, per_device(): wide = term if wide is None else wide + term  3.99 us

profile of v1, /device:TPU:1, one launch (start us, length us, event | category | flops | bytes accessed | tf_op | source)
XLA Modules:
  0.0 125.1 jit_solution(8675325893393490267)
XLA Ops:
  0.7 18.0 %shard_map.59 = (f32[4,32,384]{2,1,0:T(8,128)}, f32[4,32,384]{2,1,0:T(8,128)}, f32[4,8,8,384]{3,2,1,0:T(8,128)}, f32[4,8,384]{2,1,0:T(8,128)}, f32[4,8,384]{2,1,...) custom-call(f32[4,8,32,512]{3,2,1,0:T(8,128)} %vox.1, s32[1,32,512]{2,1,0:T(8,128)} %codes.1, ...), custom_call_target="tpu_custom_call" | custom-call | tf_op jit(solution)/shard_map/pallas_call | solution.py:87
  18.6 0.8 select_bitcast_fusion.2
  19.5 1.2 broadcast_select_fusion.1
  20.7 1.0 select_bitcast_fusion
  21.7 1.3 %constant_dynamic-slice_fusion.2 = f32[4,8,32,384]{3,2,1,0:T(8,128)} fusion(f32[4,8,32,512]{3,2,1,0:T(8,128)S(1)} %copy-done, s32[]{:T(128)S(6)} %select_n.315), kind=kLoop, calls=%fused_computation.180 | loop fusion | bytes 3145732 | tf_op jit(solution)/shard_map/dynamic_slice | solution.py:343
  23.0 0.4 iota_compare_fusion
  23.4 1.0 copy-done.1
  24.4 3.3 %fusion.7 = f32[4,10,34,258]{3,2,1,0:T(8,128)S(1)} fusion(s32[]{:T(128)S(6)} %select_n.320, f32[4,1,32,384]{3,2,1,0:T(8,128)S(1)} %get-tuple-element.156, f32[4,8,32,384]{3,2,1,0:T(8,128)S(1)} %copy-done.1, f32[4,1,32,384]{3,2,1,0:T(8,128)S(1)} %get-tuple-element.155, f32[4,10,1,384]{3,2,1,0:T(1,128)S(1)} %get-tuple-element.135, ...), kind=kLoop, calls=%fused_computation.30 | loop fusion | flops 4912320 | bytes 4195264 | tf_op jit(solution)/shard_map/concatenate | solution.py:348
  27.8 6.5 %fusion.72 = (f32[4,10,32,256]{3,2,1,0:T(8,128)}, f32[4,10,32,256]{3,2,1,0:T(8,128)}, f32[4,10,32,256]{3,2,1,0:T(8,128)}, f32[4,10,32,256]{3,2,1,0:T(8,128)}, f3...) fusion(f32[4,10,34,258]{3,2,1,0:T(8,128)S(1)} %fusion.7), kind=kLoop, calls=%fused_computation.187 | loop fusion | bytes 23592960 | tf_op jit(solution)/shard_map/slice | solution.py:356
  34.7 5.4 %multiply_add_fusion = f32[2,4,10,32,256]{4,3,2,0,1:T(8,128)S(1)} fusion(f32[4,10,32,256]{3,2,1,0:T(8,128)} %get-tuple-element.133, f32[2,32,256]{2,1,0:T(8,128)S(1)} %get-tuple-element.146, f32[4,10,32,256]{3,2,1,0:T(8,128)} %get-tuple-element.126, f32[2,32,256]{2,1,0:T(8,128)S(1)} %get-tuple-element.145, f32[4,10,32,256]{3,2,1,0:T(8,128)} %get-tuple-element.127, ...), kind=kLoop, calls=%fused_computation.25 | loop fusion | flops 11141120 | bytes 15007744 | tf_op jit(solution)/shard_map/add | solution.py:357
  41.4 0.5 fusion.70
  42.0 0.5 multiply_reduce_fusion.9
  42.5 0.6 fusion.73
  43.1 0.7 pad_slice_fusion.1
  43.8 1.7 %copy.112 = f32[128,256]{0,1:T(8,128)} copy(f32[128,256]{1,0:T(8,128)} %bitcast.173) | data formatting | bytes 262144 | tf_op jit(solution)/shard_map/squeeze | solution.py:378
  45.5 1.5 %copy.195 = f32[4,8,8,128]{3,2,0,1:T(8,128)} copy(f32[4,8,8,128]{3,2,1,0:T(8,128)} %bitcast.175) | data formatting | bytes 262144 | tf_op jit(solution)/shard_map/reshape | solution.py:311
  47.0 1.7 %copy.110 = f32[128,256]{0,1:T(8,128)} copy(f32[128,256]{1,0:T(8,128)} %bitcast.172) | data formatting | bytes 262144 | tf_op jit(solution)/shard_map/squeeze | solution.py:378
  48.7 0.9 copy.196
  49.6 1.6 %pad_maximum_fusion.im = f32[8,2,4,8,128]{4,3,2,1,0:T(8,128)} fusion(f32[8,1,4,8,128]{4,3,2,1,0:T(8,128)} %bitcast.183, f32[8,1,4,8,128]{4,3,2,1,0:T(8,128)S(1)} %bitcast.185), kind=kLoop, calls=%fused_computation.81 | loop fusion | flops 65536 | bytes 524288 | tf_op jit(solution)/shard_map/stack | solution.py:378
  51.2 0.8 pad_maximum_fusion.1
  52.1 0.6 copy.107
  52.7 1.7 %copy.108 = f32[256,128]{1,0:T(8,128)} copy(f32[256,128]{0,1:T(8,128)} %bitcast.177) | data formatting | bytes 262144 | tf_op jit(solution)/shard_map/transpose | solution.py:311
  54.4 1.5 %copy.197 = f32[4,8,8,128]{3,2,0,1:T(8,128)} copy(f32[4,8,8,128]{3,2,1,0:T(8,128)} %bitcast.178) | data formatting | bytes 262144 | tf_op jit(solution)/shard_map/reshape | solution.py:311
  56.0 0.8 fusion.49
  56.7 0.7 copy.114
  57.4 1.7 %copy.115 = s32[256,128]{1,0:T(8,128)} copy(s32[256,128]{0,1:T(8,128)} %bitcast.179) | data formatting | bytes 262144 | tf_op jit(solution)/shard_map/transpose | solution.py:311
  59.1 1.6 %copy.194 = s32[4,8,8,128]{3,2,0,1:T(8,128)} copy(s32[4,8,8,128]{3,2,1,0:T(8,128)} %bitcast.180) | data formatting | bytes 262144 | tf_op jit(solution)/shard_map/reshape | solution.py:311
  60.6 19.6 %shard_map.60 = (f32[8,4,8,128]{3,2,1,0:T(8,128)}, f32[8,128]{1,0:T(8,128)}) custom-call(f32[8,4,8,128]{3,2,1,0:T(8,128)} %bitcast.182, f32[8,2,4,8,128]{4,3,2,1,0:T(8,128)} %pad_maximum_fusion.im, s32[8,4,8,128]{3,2,1,0:T(8,128)} %bitcast.184), custom_call_target="tpu_custom_call" | custom-call | tf_op jit(solution)/shard_map/pallas_call | solution.py:245
  80.2 1.6 %copy.117 = f32[4,8,8,128]{3,2,1,0:T(8,128)} copy(f32[4,8,8,128]{3,2,0,1:T(8,128)} %bitcast.193) | data formatting | bytes 262144 | tf_op jit(solution)/shard_map/transpose | solution.py:317
  81.8 1.6 %copy.118 = f32[128,256]{1,0:T(8,128)} copy(f32[128,256]{0,1:T(8,128)} %bitcast.181) | data formatting | bytes 262144 | tf_op jit(solution)/shard_map/transpose | solution.py:317
  83.5 0.9 slice_bitcast_fusion.2
  84.3 0.5 multiply_reduce_fusion.11
  84.9 1.4 %fusion.25 = f32[2,1,8,32,256]{4,3,2,0,1:T(8,128)S(1)} fusion(f32[2,8,32,256]{3,2,1,0:T(8,128)S(1)} %get-tuple-element.119, f32[2,4,8,32,256]{4,3,2,0,1:T(8,128)S(1)} %fusion.15, f32[2,8,32,256]{3,2,1,0:T(8,128)S(1)} %fusion.67, f32[2,32,256]{2,1,0:T(8,128)S(1)} %multiply_reduce_fusion.11, f32[2,32,256]{2,1,0:T(8,128)S(1)} %get-tuple-element.140, ...), kind=kOutput, calls=%fused_computation.66 | output fusion | flops 7208960 | bytes 4096000 | tf_op jit(solution)/shard_map/jit(cumsum)/reduce_window_sum | solution.py:387
  86.3 0.5 multiply_bitcast_fusion
  86.9 0.5 subtract_multiply_fusion
  87.4 0.5 select_maximum_fusion
  88.5 4.3 %multiply_reduce_fusion.8 = (f32[4,10,32,256]{3,2,1,0:T(8,128)S(1)}, f32[4,10,32,256]{3,2,1,0:T(8,128)S(1)}, f32[4,10,32,256]{3,2,1,0:T(8,128)S(1)}, f32[4,10,32...) fusion(f32[2,32,256]{2,1,0:T(8,128)S(1)} %copy-done.22, ...), kind=kLoop, calls=%fused_computation.24 | loop fusion | flops 12124160 | bytes 20447232 | tf_op jit(solution)/shard_map/reduce_sum | solution.py:405
  92.8 4.0 %pad_add_fusion = f32[4,10,34,258]{3,2,0,1:T(8,128)S(1)} fusion(f32[4,10,32,256]{3,2,1,0:T(8,128)S(1)} %get-tuple-element.110, f32[4,10,32,256]{3,2,1,0:T(8,128)S(1)} %get-tuple-element.118, f32[4,10,32,256]{3,2,1,0:T(8,128)S(1)} %get-tuple-element.117, f32[4,10,32,256]{3,2,1,0:T(8,128)S(1)} %get-tuple-element.116, ...), kind=kLoop, calls=%fused_computation.38 | loop fusion | flops 2807040 | bytes 13200000 | tf_op jit(solution)/shard_map/add | solution.py:407
  96.8 0.6 fusion.20
  97.8 0.6 pad.72.pack
  98.6 0.6 reshape.849.line
  99.2 0.8 slice_bitcast_fusion
  100.1 18.8 %shard_map.61 = (f32[4,32,256]{2,1,0:T(8,128)}, f32[4,32,256]{2,1,0:T(8,128)}, f32[3,40,256]{2,1,0:T(8,128)}, f32[3,2,40,128]{3,2,1,0:T(8,128)}) custom-call(f32[4,32,256]{2,1,0:T(8,128)} %get-tuple-element.124.zup, f32[4,32,256]{2,1,0:T(8,128)} %get-tuple-element.123.zdn, f32[40,256]{1,0:T(8,128)} %reshape.849.line, f32[40,128]{1,0:T(8,128)} %pad.72.pack), custom_call_target="tpu_custom_call" | custom-call | tf_op jit(solution)/shard_map/pallas_call | solution.py:285
  118.9 0.9 reshape.852
  120.0 1.0 copy.144
  122.5 0.9 add_select_fusion
  123.3 1.0 copy.150
  124.5 0.6 copy.149
  (105 shorter events, 4.2 us)
Async XLA Ops:
  0.6 21.0 %copy-start = (f32[4,8,32,512]{3,2,1,0:T(8,128)S(1)}, f32[4,8,32,512]{3,2,1,0:T(8,128)}, u32[]{:S(2)}) copy-start(f32[4,8,32,512]{3,2,1,0:T(8,128)} %vox.1) | copy-start | bytes 6291460
  23.0 1.4 %copy-start.1 = (f32[4,8,32,384]{3,2,1,0:T(8,128)S(1)}, f32[4,8,32,384]{3,2,1,0:T(8,128)}, u32[]{:S(2)}) copy-start(f32[4,8,32,384]{3,2,1,0:T(8,128)} %constant_dynamic-slice_fusion.2) | copy-start | bytes 4718596
  27.8 6.5 %copy-start.25 = (s32[1,32,512]{2,1,0:T(8,128)S(1)}, s32[1,32,512]{2,1,0:T(8,128)}, u32[]{:S(2)}) copy-start(s32[1,32,512]{2,1,0:T(8,128)} %codes.1) | copy-start | bytes 196612
  27.8 6.5 %copy-start.26 = (s32[1,32,512]{2,1,0:T(8,128)S(1)}, s32[1,32,512]{2,1,0:T(8,128)}, u32[]{:S(2)}) copy-start(s32[1,32,512]{2,1,0:T(8,128)} %head.1) | copy-start | bytes 196612
  27.8 6.6 %copy-start.27 = (s32[32,256]{1,0:T(8,128)S(1)}, s32[32,256]{1,0:T(8,128)}, u32[]{:S(2)}) copy-start(s32[32,256]{1,0:T(8,128)} %get-tuple-element.88) | copy-start | bytes 98308
  34.3 7.1 %copy-start.24 = (s32[1,32,256]{2,1,0:T(8,128)}, s32[1,32,256]{2,1,0:T(8,128)S(1)}, u32[]{:S(2)}) copy-start(s32[1,32,256]{2,1,0:T(8,128)S(1)} %get-tuple-element.159) | copy-start | bytes 98308
  34.5 5.6 %copy-start.21 = (f32[2,32,256]{2,1,0:T(8,128)}, f32[2,32,256]{2,1,0:T(8,128)S(1)}, u32[]{:S(2)}) copy-start(f32[2,32,256]{2,1,0:T(8,128)S(1)} %get-tuple-element.153) | copy-start | bytes 196612
  34.5 5.7 %copy-start.15 = (f32[2,32,256]{2,1,0:T(8,128)}, f32[2,32,256]{2,1,0:T(8,128)S(1)}, u32[]{:S(2)}) copy-start(f32[2,32,256]{2,1,0:T(8,128)S(1)} %get-tuple-element.150) | copy-start | bytes 196612
  34.5 5.7 %copy-start.17 = (f32[2,32,256]{2,1,0:T(8,128)}, f32[2,32,256]{2,1,0:T(8,128)S(1)}, u32[]{:S(2)}) copy-start(f32[2,32,256]{2,1,0:T(8,128)S(1)} %get-tuple-element.151) | copy-start | bytes 196612
  34.5 5.7 %copy-start.19 = (f32[2,32,256]{2,1,0:T(8,128)}, f32[2,32,256]{2,1,0:T(8,128)S(1)}, u32[]{:S(2)}) copy-start(f32[2,32,256]{2,1,0:T(8,128)S(1)} %get-tuple-element.152) | copy-start | bytes 196612
  34.7 5.5 %copy-start.3 = (f32[2,32,256]{2,1,0:T(8,128)}, f32[2,32,256]{2,1,0:T(8,128)S(1)}, u32[]{:S(2)}) copy-start(f32[2,32,256]{2,1,0:T(8,128)S(1)} %get-tuple-element.144) | copy-start | bytes 196612
  34.7 5.5 %copy-start.5 = (f32[2,32,256]{2,1,0:T(8,128)}, f32[2,32,256]{2,1,0:T(8,128)S(1)}, u32[]{:S(2)}) copy-start(f32[2,32,256]{2,1,0:T(8,128)S(1)} %get-tuple-element.145) | copy-start | bytes 196612
  34.7 5.5 %copy-start.7 = (f32[2,32,256]{2,1,0:T(8,128)}, f32[2,32,256]{2,1,0:T(8,128)S(1)}, u32[]{:S(2)}) copy-start(f32[2,32,256]{2,1,0:T(8,128)S(1)} %get-tuple-element.146) | copy-start | bytes 196612
  34.7 5.5 %copy-start.9 = (f32[2,32,256]{2,1,0:T(8,128)}, f32[2,32,256]{2,1,0:T(8,128)S(1)}, u32[]{:S(2)}) copy-start(f32[2,32,256]{2,1,0:T(8,128)S(1)} %get-tuple-element.147) | copy-start | bytes 196612
  34.7 5.5 %copy-start.11 = (f32[2,32,256]{2,1,0:T(8,128)}, f32[2,32,256]{2,1,0:T(8,128)S(1)}, u32[]{:S(2)}) copy-start(f32[2,32,256]{2,1,0:T(8,128)S(1)} %get-tuple-element.148) | copy-start | bytes 196612
  34.7 5.5 %copy-start.13 = (f32[2,32,256]{2,1,0:T(8,128)}, f32[2,32,256]{2,1,0:T(8,128)S(1)}, u32[]{:S(2)}) copy-start(f32[2,32,256]{2,1,0:T(8,128)S(1)} %get-tuple-element.149) | copy-start | bytes 196612
  40.3 1.1 copy-start.30
  40.6 1.3 %copy-start.23 = (f32[1,3,32,512]{3,2,1,0:T(8,128)S(1)}, f32[1,3,32,512]{3,2,1,0:T(8,128)}, u32[]{:S(2)}) copy-start(f32[1,3,32,512]{3,2,1,0:T(8,128)} %cot.1) | copy-start | bytes 589828
  40.6 1.3 %copy-start.2 = (f32[3,32,256]{2,1,0:T(8,128)S(1)}, f32[3,32,256]{2,1,0:T(8,128)}, u32[]{:S(2)}) copy-start(f32[3,32,256]{2,1,0:T(8,128)} %get-tuple-element.94) | copy-start | bytes 294916
  87.3 0.8 copy-start.4
  87.3 0.9 copy-start.6
  87.3 0.9 copy-start.8
  87.4 0.9 copy-start.10
  87.4 0.9 copy-start.12
  87.4 1.0 copy-start.14
  87.4 1.0 copy-start.16
  87.4 1.0 copy-start.18
  87.4 1.0 copy-start.20
  87.4 1.0 copy-start.22
  121.3 0.9 copy-start.29
  121.3 1.0 copy-start.28
  121.4 0.5 copy-start.32
  122.5 1.9 %copy-start.31 = (f32[8,128]{1,0:T(8,128)S(1)}, f32[8,128]{1,0:T(8,128)}, u32[]{:S(2)}) copy-start(f32[8,128]{1,0:T(8,128)} %get-tuple-element.96) | copy-start | bytes 12292

commit v2 on v0

v2 whole, which is shorter than its diff:
```python
import functools
from types import SimpleNamespace
from typing import NamedTuple

import jax
import jax.numpy as jnp
from jax import lax
from jax.experimental import pallas as pl
from jax.experimental.pallas import tpu as pltpu
from jax.sharding import Mesh
from jax.sharding import PartitionSpec as P

LEVELS = 8
AXES = ("dir", "sy", "sx", "sz", "tile")
SLAB = AXES[1:4]
MESH = pl.DeviceIdType.MESH
ANY = pl.BlockSpec(memory_space=pl.ANY)
VM = pl.BlockSpec(memory_space=pltpu.VMEM)


class Place(NamedTuple):
    dir: int
    sy: int
    sx: int
    sz: int
    tile: int


def places():
    return Place(*[lax.axis_index(a) for a in AXES])


def slab_index(me):
    _, _, sx, sz, _ = (lax.axis_size(a) for a in AXES)
    return (me.sy * sx + me.sx) * sz + me.sz


def at_slab(me, step):
    sy, sx, sz = (lax.axis_size(a) for a in SLAB)
    s = lax.rem(slab_index(me) + step + sy * sx * sz, sy * sx * sz)
    return me._replace(sy=s // (sx * sz), sx=(s // sz) % sx, sz=s % sz)


def greet(peers):
    barrier = pltpu.get_barrier_semaphore()
    for peer in peers:
        pl.semaphore_signal(barrier, inc=1, device_id=tuple(peer), device_id_type=MESH)
    pl.semaphore_wait(barrier, len(peers))


def push(src, dst, send, recv, peer):
    return pltpu.make_async_remote_copy(
        src_ref=src, dst_ref=dst, send_sem=send, recv_sem=recv,
        device_id=tuple(peer), device_id_type=MESH,
    )


def shapes(ch, planes, rows, half, wide, nz, ng):
    lanes, m = 4 * rows, half // 8 // nz
    ext = planes + 2
    f32 = jnp.float32
    one = dict(
        grid=(ch, ext, rows, half), wing=(ch, ext, rows, wide),
        rows=(ch, ext, 8, half), rwing=(ch, ext, 8, wide),
        plane=(2, ch, ext, rows, half), sigma=(2, planes, rows, half),
        slope=(2, planes, rows, half), colour=(2, 3, planes, rows, half),
        through=(2, planes, rows, half), glow=(2, planes, rows, half),
        taps=(2, 9, rows, half), pair=(2, 7, rows, half),
        codes=(2, rows, half), heading=(2, rows, half), pull=(2, 3, rows, half),
        ahead=(2, planes, rows, half), stack=(lanes, half),
        diff=(2, ch, planes + 4, rows, half), out=(ch, ext, rows, half),
        line=(ext, ch, half), pack=(rows + 8, max(wide, ch * ext)),
        fp=(ch, rows, half), fn=(ch, rows, half),
        rline=(3, ext, ch, half), rpack=(3, 2, rows + 8, max(wide, ch * ext)),
        tile=(wide, lanes),
        dl=(nz, m, 8, lanes), im=(nz, 2, m, 8, lanes), hd=(nz, m, 8, lanes),
        rdl=(nz, m, 8, lanes), rim=(nz, 2, m, 8, lanes), gm=(ng, m, 8, lanes),
        ret=(nz, m, 8, lanes), rb=(nz, m, 8, lanes),
        part=(2, m, 8, lanes), rpart=(ng, 8, lanes),
    )
    ints = dict(codes=0, heading=0)
    return {k: pltpu.VMEM(v, jnp.int32 if k in ints else f32) for k, v in one.items()}


def weights(b, g):
    level = LEVELS
    q = b.codes[g]
    frac = lambda raw: (raw.astype(jnp.float32) + 0.5) / level - 0.5
    fz, fy, fx = frac(q & 7), frac((q >> 3) & 7), frac(q >> 6)
    three = lambda f: (jnp.maximum(-f, 0.0), 1.0 - jnp.abs(f), jnp.maximum(f, 0.0))
    wy, wx = three(fy), three(fx)
    for i in range(3):
        for j in range(3):
            b.taps[g, 3 * i + j] = wy[i] * wx[j]
    ay, ax = jnp.abs(fy), jnp.abs(fx)
    for i, v in enumerate((fz, fy, fx, wy[1] * wx[1], wy[1] * ax, ay * wx[1], ay * ax)):
        b.pair[g, i] = v


def iota(shape, dim):
    return lax.broadcasted_iota(jnp.int32, shape, dim)


def sample_plane(b, me, p, keep):
    ch, _, rows, half = b.grid.shape
    tw = half // 2
    d, t = me.dir, me.tile
    row, lane = iota((rows, tw), 0), iota((rows, tw), 1)
    right = (d == 0).astype(jnp.float32)
    left = 1.0 - right
    under = (t == 0).astype(jnp.float32)
    over = 1.0 - under
    for c in range(ch):
        pick = lambda r: jnp.where(d == 0, r[:, 0:1], r[:, tw - 1:tw])
        edge = jnp.broadcast_to(pick(b.wing[c, p]), (rows, tw))
        fr = lambda r: jnp.where(t == 0, r[0:1], r[7:8])
        ecorner = jnp.broadcast_to(pick(fr(b.rwing[c, p])), (1, tw))
        m = [b.grid[c, p, :, x * tw:(x + 1) * tw] for x in range(2)] + [edge]
        far = [fr(b.rows[c, p, :, x * tw:(x + 1) * tw]) for x in range(2)] + [ecorner]
        up = [jnp.where(row == 0, f * over, pltpu.roll(a, 1, 0)) for a, f in zip(m, far)]
        dn = [jnp.where(row == rows - 1, f * under, pltpu.roll(a, rows - 1, 0))
              for a, f in zip(m, far)]
        spread = []
        for a in (up, m, dn):
            r = [pltpu.roll(a[x], 1, 1) for x in range(2)]
            l = [pltpu.roll(a[x], tw - 1, 1) for x in range(2)]
            lo = [jnp.where(lane == 0, a[2] * left, r[0]), jnp.where(lane == 0, r[0], r[1])]
            hi = [jnp.where(lane == tw - 1, l[1], l[0]),
                  jnp.where(lane == tw - 1, a[2] * right, l[1])]
            spread.append((lo, a[:2], hi))
        for x in range(2):
            at = slice(x * tw, (x + 1) * tw)
            for g in range(2):
                fy, fx = b.pair[g, 1, :, at], b.pair[g, 2, :, at]
                w00, w01 = b.pair[g, 3, :, at], b.pair[g, 4, :, at]
                w10, w11 = b.pair[g, 5, :, at], b.pair[g, 6, :, at]
                side = lambda s: jnp.where(fx > 0, s[2][x], s[0][x])
                down = fy > 0
                v = (w00 * m[x] + w01 * side(spread[1])
                     + w10 * jnp.where(down, dn[x], up[x])
                     + w11 * jnp.where(down, side(spread[2]), side(spread[0])))
                b.plane[g, c, p, :, at] = v if keep is None else v * keep


def shade_planes(b, scale):
    _, ch, ext, rows, half = b.plane.shape
    planes = ext - 2

    def step(k, acc):
        new = []
        for g in range(2):
            fz = b.pair[g, 0]
            az = jnp.abs(fz)
            v = []
            for c in range(ch):
                mid = b.plane[g, c, k + 1]
                far = jnp.where(fz > 0, b.plane[g, c, k + 2], b.plane[g, c, k])
                v.append((1.0 - az) * mid + az * far)
            sg = (jnp.maximum(v[0], 0.0) + jnp.log(1.0 + jnp.exp(-jnp.abs(v[0])))) * scale
            b.sigma[g, k] = sg
            b.slope[g, k] = (0.5 + 0.5 * jnp.tanh(0.5 * v[0])) * scale
            for c in range(3):
                b.colour[g, c, k] = 0.5 + 0.5 * jnp.tanh(0.5 * v[c + 1])
            b.ahead[g, k] = acc[g]
            new.append(acc[g] + sg)
        return tuple(new)

    zero = jnp.zeros((rows, half), jnp.float32)
    return lax.fori_loop(0, planes, step, (zero, zero))


def local_light(b, totals):
    _, planes, rows, half = b.sigma.shape
    images = []
    for g in range(2):
        forward = b.heading[g] == 0

        def step(k, acc):
            sg, ah = b.sigma[g, k], b.ahead[g, k]
            front = jnp.where(forward, ah, totals[g] - ah - sg)
            th = jnp.exp(-front)
            gl = th * (1.0 - jnp.exp(-sg))
            b.through[g, k] = th
            b.glow[g, k] = gl
            return tuple(acc[c] + gl * b.colour[g, c, k] for c in range(3))

        zero = jnp.zeros((rows, half), jnp.float32)
        images.append(lax.fori_loop(0, planes, step, (zero,) * 3))
    return images


def tiles_out(b, put, nz):
    lanes, half = b.stack.shape
    tw = half // 2
    for x in range(2):
        turned = b.stack[:, x * tw:(x + 1) * tw].T
        for i in range(tw // 8):
            j = x * (tw // 8) + i
            put(j % nz, j // nz, turned[8 * i:8 * i + 8])


def backward(b, kept):
    _, planes, rows, half = b.sigma.shape
    zero = jnp.zeros((rows, half), jnp.float32)
    for g in range(2):
        forward = b.heading[g] == 0
        reach = b.stack[2 * g * rows:(2 * g + 1) * rows]
        rest = b.stack[(2 * g + 1) * rows:(2 * g + 2) * rows]
        whole = reach * kept[g]
        for c in range(4):
            for k in (0, 1, planes + 2, planes + 3):
                b.diff[g, c, k] = zero

        def step(k, before):
            pull = [b.pull[g, c] for c in range(3)]
            col = [b.colour[g, c, k] for c in range(3)]
            shade = pull[0] * col[0] + pull[1] * col[1] + pull[2] * col[2]
            th, gl = b.through[g, k], b.glow[g, k]
            lit = reach * gl
            share = lit * shade
            behind = rest + jnp.where(forward, whole - before - share, before)
            b.diff[g, 0, k + 2] = (reach * (th - gl) * shade - behind) * b.slope[g, k]
            for c in range(3):
                b.diff[g, c + 1, k + 2] = pull[c] * lit * (col[c] * (1.0 - col[c]))
            return before + share

        lax.fori_loop(0, planes, step, zero)


def spill_plane(b, me, p):
    ch, ext, rows, half = b.out.shape
    tw = half // 2
    d, t = me.dir, me.tile
    row, lane = iota((rows, tw), 0), iota((rows, tw), 1)
    for c in range(ch):
        pos = c * ext + p
        cols = []
        for g in range(2):
            fz = b.pair[g, 0]
            cols.append((1.0 - jnp.abs(fz)) * b.diff[g, c, p + 1]
                        + jnp.maximum(fz, 0.0) * b.diff[g, c, p]
                        + jnp.maximum(-fz, 0.0) * b.diff[g, c, p + 2])
        bands = []
        for i in range(3):
            u = []
            for j in range(3):
                full = (b.taps[0, 3 * i + j] * cols[0] + b.taps[1, 3 * i + j] * cols[1])
                u.append([full[:, :tw], full[:, tw:]])
            l = [pltpu.roll(a, tw - 1, 1) for a in u[0]]
            r = [pltpu.roll(a, 1, 1) for a in u[2]]
            x0 = u[1][0] + jnp.where(lane == tw - 1, l[1], l[0]) + jnp.where(lane == 0, 0.0, r[0])
            x1 = u[1][1] + jnp.where(lane == tw - 1, 0.0, l[1]) + jnp.where(lane == 0, r[0], r[1])
            bands.append([x0, x1, jnp.where(d == 0, r[1], u[0][0])])
        done, far = [], []
        for x in range(3):
            up = pltpu.roll(bands[0][x], rows - 1, 0)
            dn = pltpu.roll(bands[2][x], 1, 0)
            done.append(bands[1][x] + jnp.where(row == rows - 1, 0.0, up)
                        + jnp.where(row == 0, 0.0, dn))
            far.append(jnp.where(t == 0, dn[0:1], up[rows - 1:rows]))
        b.out[c, p, :, :tw] = done[0]
        b.out[c, p, :, tw:] = done[1]
        b.line[p, c:c + 1, :tw] = far[0]
        b.line[p, c:c + 1, tw:] = far[1]
        slot = iota((rows, b.pack.shape[1]), 1)
        wide = b.pack.shape[1]
        b.pack[:rows] = jnp.where(
            slot == pos, jnp.broadcast_to(done[2][:, 0:1], (rows, wide)), b.pack[:rows])
        b.pack[rows:rows + 1] = jnp.where(
            slot[0:1] == pos, jnp.broadcast_to(far[2][:, 0:1], (1, wide)), b.pack[rows:rows + 1])


def gather_spill(b, me, has_prev, has_next, dest):
    ch, ext, rows, half = b.out.shape
    planes = ext - 2
    tw = half // 2
    wide = b.pack.shape[1]
    d, t = me.dir, me.tile
    touch = (1 - t) * (rows - 1)
    seam = (1 - d) * (half - 1)
    slot = iota((rows, wide), 1)
    row = iota((rows, tw), 0)
    lane = iota((rows, tw), 1)

    def merged(i, lo, hi):
        a = b.rpack[1, i, lo:hi]
        at = slot[:hi - lo] % ext
        a = a + jnp.where(at == 1, pltpu.roll(b.rpack[0, i, lo:hi], wide - planes, 1), 0.0) * has_prev
        return a + jnp.where(at == planes, pltpu.roll(b.rpack[2, i, lo:hi], planes, 1), 0.0) * has_next

    col = merged(0, 0, rows)
    corner = merged(1, rows, rows + 8)[0:1]
    col = col + jnp.where(iota((rows, wide), 0) == touch, jnp.broadcast_to(corner, (rows, wide)), 0.0)
    for c in range(ch):
        for k in range(planes):
            pos = c * ext + k + 1
            extra = b.rline[1, k + 1, c:c + 1]
            v = b.out[c, k + 1]
            if k == 0:
                extra = extra + b.rline[0, ext - 1, c:c + 1] * has_prev
                v = v + b.fp[c] * has_prev
            if k == planes - 1:
                extra = extra + b.rline[2, 0, c:c + 1] * has_next
                v = v + b.fn[c] * has_next
            bar = jnp.broadcast_to(col[:, pos:pos + 1], (rows, tw))
            for x in range(2):
                at = slice(x * tw, (x + 1) * tw)
                y = v[:, at] + jnp.where(row == touch, jnp.broadcast_to(extra[:, at], (rows, tw)), 0.0)
                y = y + jnp.where(lane + x * tw == seam, bar, 0.0)
                dest[c, k, :, at] = y


def render_kernel(scale, depth, names, vox, codes, head, cot, grad, img, *scratch):
    b = SimpleNamespace(**dict(zip(names, scratch)))
    sems = scratch[len(names):]
    (lsem, hs, hr, s1, r1, s2, r2, s3, r3, s4, r4, s5, r5, ss, sr) = sems
    me = places()
    nsy, nsx, nz = (lax.axis_size(a) for a in SLAB)
    ng = nsy * nsx
    blocks = ng // 2
    d, t, z = me.dir, me.tile, me.sz
    gi = me.sy * nsx + me.sx
    s = slab_index(me)
    prev, nxt = at_slab(me, -1), at_slab(me, 1)
    flip = lambda p: p._replace(tile=1 - p.tile)
    over = lambda p: p._replace(dir=1 - p.dir)
    near = [prev, me, nxt]
    mate = me._replace(dir=1 - d, sx=nsx - 1 - me.sx)
    ch, ext, rows, half = b.grid.shape
    planes = ext - 2
    wide = b.wing.shape[-1]
    has_prev = (s > 0).astype(jnp.float32)
    has_next = (s < nsy * nsx * nz - 1).astype(jnp.float32)

    mine = pl.ds(pl.multiple_of(d * half, half), half)
    theirs = pl.ds(pl.multiple_of((1 - d) * half, half), half)
    beside = pl.ds(pl.multiple_of(half - d * wide, wide), wide)
    loads = [
        (vox.at[:, :, :, mine], b.grid.at[:, 1:planes + 1]),
        (vox.at[:, :, :, beside], b.wing.at[:, 1:planes + 1]),
        (codes.at[0, :, mine], b.codes.at[0]),
        (head.at[0, :, mine], b.heading.at[0]),
        (cot.at[0, :, :, mine], b.pull.at[0]),
    ]
    loads = [pltpu.make_async_copy(a, c, lsem.at[i]) for i, (a, c) in enumerate(loads)]
    for c in loads:
        c.start()

    zpeer = [me._replace(sz=lax.rem(z + i, nz)) for i in range(1, nz)]
    gpeer, across = [], []
    for i in range(ng):
        g = lax.rem(gi + i, ng)
        p = me._replace(sy=g // nsx, sx=g % nsx)
        across.append(over(p))
        if i:
            gpeer.append(p)
    greet([prev, nxt] + [flip(p) for p in near] + [over(p) for p in near]
          + [over(flip(p)) for p in near] + zpeer + gpeer + across)

    rays = [
        (codes.at[0, :, theirs], b.codes.at[1], mate),
        (head.at[0, :, theirs], b.heading.at[1], mate),
        (cot.at[0, :, :, theirs], b.pull.at[1], mate),
    ]
    rays = [push(x, y, hs.at[i], hr.at[i], p) for i, (x, y, p) in enumerate(rays)]
    for c in rays:
        c.start()
    for c in loads[:2]:
        c.wait()
    edge = pl.ds(pl.multiple_of((1 - t) * (rows - 8), 8), 8)
    inner = pl.ds(1, planes)
    beyond = [
        (b.grid.at[:, inner, edge], b.rows.at[:, inner], flip(me)),
        (b.wing.at[:, inner, edge], b.rwing.at[:, inner], flip(me)),
        (b.grid.at[:, planes], b.grid.at[:, 0], nxt),
        (b.grid.at[:, 1], b.grid.at[:, ext - 1], prev),
        (b.wing.at[:, planes], b.wing.at[:, 0], nxt),
        (b.wing.at[:, 1], b.wing.at[:, ext - 1], prev),
        (b.grid.at[:, planes, edge], b.rows.at[:, 0], flip(nxt)),
        (b.grid.at[:, 1, edge], b.rows.at[:, ext - 1], flip(prev)),
        (b.wing.at[:, planes, edge], b.rwing.at[:, 0], flip(nxt)),
        (b.wing.at[:, 1, edge], b.rwing.at[:, ext - 1], flip(prev)),
    ]
    beyond = [push(x, y, hs.at[3 + i], hr.at[3 + i], p) for i, (x, y, p) in enumerate(beyond)]
    for c in beyond:
        c.start()
    for c in loads[2:]:
        c.wait()
    weights(b, 0)
    rays[0].wait()
    weights(b, 1)
    for c in beyond[:2]:
        c.wait()

    def inside(p, carry):
        sample_plane(b, me, p, None)
        return carry

    lax.fori_loop(1, planes + 1, inside, 0)
    for c in beyond[2:]:
        c.wait()

    def ends(i, carry):
        sample_plane(b, me, i * (ext - 1), jnp.where(i == 0, has_prev, has_next))
        return carry

    lax.fori_loop(0, 2, ends, 0)
    totals = shade_planes(b, scale)
    for c in rays[1:]:
        c.wait()
    for g in range(2):
        for c in range(3):
            b.pull[g, c] = b.pull[g, c] * depth
    images = local_light(b, totals)
    kept = []
    for g in range(2):
        kept.append(sum(b.pull[g, c] * images[g][c] for c in range(3)))
        b.stack[2 * g * rows:(2 * g + 1) * rows] = totals[g]
        b.stack[(2 * g + 1) * rows:(2 * g + 2) * rows] = kept[g]

    def put_dl(j, m, v):
        b.dl[j, m] = v

    tiles_out(b, put_dl, nz)
    first = [push(b.dl.at[p.sz], b.rdl.at[z], s1.at[i], r1.at[i], p)
             for i, p in enumerate(zpeer)]
    for c in first:
        c.start()
    for g in range(2):
        for c in range(3):
            b.stack[c * rows:(c + 1) * rows] = images[g][c]

        def put_im(j, m, v):
            b.im[j, g, m] = v

        tiles_out(b, put_im, nz)
    late = [push(b.im.at[p.sz], b.rim.at[z], s2.at[i], r2.at[i], p)
            for i, p in enumerate(zpeer)]
    for c in late:
        c.start()
    for g in range(2):
        for i in range(2):
            b.stack[(2 * g + i) * rows:(2 * g + i + 1) * rows] = b.heading[g].astype(jnp.float32)

    def put_hd(j, m, v):
        b.hd[j, m] = v

    tiles_out(b, put_hd, nz)
    b.rdl[z] = b.dl[z]
    b.rim[z] = b.im[z]
    lanes = b.dl.shape[-1]
    ahead = b.hd[z] == 0
    spot = iota(ahead.shape, 2)
    is_d = (spot // rows) % 2 == 0
    for c in first:
        c.wait()
    roll = lambda a, n: pltpu.roll(a, n % lanes, 2)

    def directed(parts):
        lows, low = [], jnp.zeros_like(parts[0])
        for p in parts:
            lows.append(low)
            low = low + p
        highs, high = [], jnp.zeros_like(parts[0])
        for p in reversed(parts):
            highs.append(high)
            high = high + p
        highs = highs[::-1]
        before = [jnp.where(ahead, x, y) for x, y in zip(lows, highs)]
        after = [jnp.where(ahead, y, x) for x, y in zip(lows, highs)]
        return before, after, low

    tiles = [b.rdl[i] for i in range(nz)]
    before, _, dsum = directed(tiles)
    reach = [jnp.exp(-x) for x in before]
    pulled = [roll(r, rows) * x for r, x in zip(reach, tiles)]
    _, behind, lsum = directed(pulled)
    b.gm[gi] = jnp.where(is_d, dsum, lsum)
    second = [push(b.gm.at[gi], b.gm.at[gi], s3.at[i], r3.at[i], p)
              for i, p in enumerate(gpeer)]
    for c in second:
        c.start()
    for c in second:
        c.wait()
    groups = [b.gm[i] for i in range(ng)]
    gbefore, _, _ = directed(groups)
    greach = [jnp.exp(-x) for x in gbefore]
    gpull = [roll(r, rows) * x for r, x in zip(greach, groups)]
    _, gafter, _ = directed(gpull)
    to_me = jnp.zeros_like(dsum)
    rest = jnp.zeros_like(dsum)
    for i in range(ng):
        to_me = jnp.where(gi == i, greach[i], to_me)
        rest = jnp.where(gi == i, gafter[i], rest)
    to_me_l = roll(to_me, rows)
    full = []
    for i in range(nz):
        r = to_me * reach[i]
        full.append(r)
        b.ret[i] = jnp.where(is_d, r, rest + to_me_l * behind[i])
    back = [push(b.ret.at[p.sz], b.rb.at[z], s4.at[i], r4.at[i], p)
            for i, p in enumerate(zpeer)]
    for c in back:
        c.start()
    b.rb[z] = b.ret[z]
    for c in late:
        c.wait()
    quarter = spot // rows
    for g in range(2):
        total = jnp.zeros_like(dsum)
        for i in range(nz):
            src = full[i]
            wash = roll(src, -2 * g * rows)
            wash = jnp.where(quarter == 1, roll(src, (1 - 2 * g) * rows), wash)
            wash = jnp.where(quarter == 2, roll(src, (2 - 2 * g) * rows), wash)
            total = total + wash * b.rim[i, g]
        b.part[g] = total
    half_of_me = gi // blocks
    out = []
    for g in range(2):
        for m in range(blocks):
            q = blocks * d + m
            peer = me._replace(dir=d if g == 0 else 1 - d, sy=q // nsx, sx=q % nsx)
            out.append(push(b.part.at[g, m], b.rpart.at[gi],
                            s5.at[g * blocks + m], r5.at[gi], peer))
    for g in range(2):
        for m in range(blocks):
            copy = out[g * blocks + m]
            if g == 0:
                itself = gi == blocks * d + m

                @pl.when(itself)
                def _():
                    b.rpart[gi] = b.part[0, m]

                @pl.when(jnp.logical_not(itself))
                def _():
                    copy.start()
            else:
                copy.start()
    for c in back:
        c.wait()

    tw = half // 2
    for x in range(2):
        for i in range(tw // 8):
            j = x * (tw // 8) + i
            b.tile[8 * i:8 * i + 8] = b.rb[j % nz, j // nz]
        b.stack[:, x * tw:(x + 1) * tw] = b.tile[...].T
    backward(b, kept)

    def spread(p, carry):
        spill_plane(b, me, p)
        return carry

    lax.fori_loop(0, ext, spread, 0)
    spill = [(b.out.at[:, ext - 1], b.fp, nxt), (b.out.at[:, 0], b.fn, prev)]
    for i, p in enumerate(near):
        spill.append((b.line, b.rline.at[2 - i], flip(p)))
    for i, p in enumerate(near):
        spill.append((b.pack, b.rpack.at[2 - i, 0], over(p)))
        spill.append((b.pack, b.rpack.at[2 - i, 1], over(flip(p))))
    spill = [push(x, y, ss.at[i], sr.at[i], p) for i, (x, y, p) in enumerate(spill)]
    for c in spill:
        c.start()

    for g in range(2):
        for m in range(blocks):
            copy = out[g * blocks + m]
            if g == 0:
                @pl.when(gi != blocks * d + m)
                def _():
                    copy.wait_send()
            else:
                copy.wait_send()
    for i in range(ng):
        arrive = push(b.part.at[0, 0], b.rpart.at[i], s5.at[0], r5.at[i], over(me))

        @pl.when(jnp.logical_or(half_of_me != d, gi != i))
        def _():
            arrive.wait_recv()
    total = b.rpart[0]
    for i in range(1, ng):
        total = total + b.rpart[i]
    img[...] = total
    for c in spill:
        c.wait()
    gather_spill(b, me, has_prev, has_next, grad)


def per_device(voxels, offsets, heading, cotangent):
    ch, planes, rows, total = voxels.shape
    nsy, nsx, nz = (lax.axis_size(a) for a in SLAB)
    ng = nsy * nsx
    depth = planes * nz * ng
    half = total // 2
    wide = half // 2
    room = shapes(ch, planes, rows, half, wide, nz, ng)
    dma = lambda n: pltpu.SemaphoreType.DMA((n,))
    grad, img = pl.pallas_call(
        functools.partial(render_kernel, 2.0 / depth, float(depth), tuple(room)),
        out_shape=(jax.ShapeDtypeStruct((ch, planes, rows, half), jnp.float32),
                   jax.ShapeDtypeStruct((8, 4 * rows), jnp.float32)),
        in_specs=[ANY] * 4,
        out_specs=(VM, VM),
        scratch_shapes=list(room.values()) + [
            dma(5), dma(13), dma(13),
            dma(nz - 1), dma(nz - 1), dma(nz - 1), dma(nz - 1),
            dma(ng - 1), dma(ng - 1), dma(nz - 1), dma(nz - 1),
            dma(ng), dma(ng), dma(11), dma(11),
        ],
        compiler_params=pltpu.CompilerParams(
            collective_id=0, has_side_effects=True, vmem_limit_bytes=60 * 1024 * 1024
        ),
    )(voxels, offsets, heading, cotangent)
    image = img.T.reshape(4, rows, 8)[None, :3]
    return (image, grad)


def solution(mesh):
    n = mesh.devices.size
    shape = (2, 4, 2, 8, 2) if n == 256 else (2, 2, 1, 2, 2)
    finer = Mesh(mesh.devices.reshape(shape), AXES)
    return jax.shard_map(
        per_device,
        mesh=finer,
        in_specs=(
            P(None, SLAB, "tile", None),
            P("dir", "tile", None),
            P("dir", "tile", None),
            P("dir", None, "tile", None),
        ),
        out_specs=(P("dir", None, "tile", SLAB), P(None, SLAB, "tile", "dir")),
        check_vma=False,
    )
```

time: 266 us -> 59.4 us (0.22)
  blocking collectives: 102 us -> 0 us
  starting transfers between devices: 68 us -> 0 us
  Pallas kernels: 0 us -> 54.9 us
  other arithmetic: 53.2 us -> 0 us
  waiting for transfers between devices: 26.6 us -> 0 us
  local copies, waits for them, and re-layouts: 13.8 us -> 3.67 us
    all_gather x10 -> x0, blocking collectives: 102 us -> none  [prefix_by_axis(): pieces = lax.all_gather(subtotal, axis)]
    pallas_call x0 -> x1, Pallas kernels: none -> 54.9 us  [per_device(): pl.pallas_call(functools.partial(render_kernel, 2.0 / depth, float(depth)...]
    ppermute x10 -> x0, starting transfers between devices: 50.7 us -> none  [the longest x5 41.2 us: padded(): lax.ppermute(lax.slice_in_dim(block, 0, width, axis=dim), axis, backward)]
    all_to_all x2 -> x0, waiting for transfers between devices: 23.7 us -> none  [sent_and_summed(): lax.all_to_all(blocks, axis, split_axis=0, concat_axis=0, tiled=True)]
    all_to_all x2 -> x0, starting transfers between devices: 17.3 us -> none  [sent_and_summed(): lax.all_to_all(blocks, axis, split_axis=0, concat_axis=0, tiled=True)]
    add x11 -> x0, other arithmetic: 13.6 us -> none  [the longest x1 8.28 us: per_device(): plane = term if plane is None else plane + term]
    concatenate x4 -> x0, other arithmetic: 11.1 us -> none  [padded(): block = jnp.concatenate([low, block, high], axis=dim)]
    reduce_sum x5 -> x0, other arithmetic: 9.09 us -> none  [the longest x1 3.34 us: per_device(): shade = jnp.sum(pull[:, :, None] * colour, axis=1)]
  transfers between devices with their start and end apart: 12 -> 0, of which waited for: 2 -> 0; matrix products, arithmetic and copies ran while one was open for 11% -> 0% of each run, Pallas kernels for 0% -> 0%
where the time goes in v2:
time: 59.4 us; the launch traced here: 59.2 us
  Pallas kernels  54.9 us (92%)
  local copies, waits for them, and re-layouts  3.67 us (6%)
  between operations  0.64 us (1%)
    pallas_call x1, Pallas kernels, per_device(): pl.pallas_call(functools.partial(render_kernel, 2.0 / depth, float(depth)...  54.9 us
    unnamed x2, local copies, waits for them, and re-layouts  2.91 us

profile of v2, /device:TPU:1, one launch (start us, length us, event | category | flops | bytes accessed | tf_op | source)
XLA Modules:
  0.0 59.2 jit_solution(235695623270633436)
XLA Ops:
  0.6 54.9 %shard_map.59 = (f32[4,8,32,256]{3,2,1,0:T(8,128)}, f32[8,128]{1,0:T(8,128)}) custom-call(f32[4,8,32,512]{3,2,1,0:T(8,128)} %vox.1, s32[1,32,512]{2,1,0:T(8,128)} %codes.1, s32[1,32,512]{2,1,0:T(8,128)} %head.1, f32[1,3,32,512]{3,2,1,0:T(8,128)} %cot.1), custom_call_target="tpu_custom_call" | custom-call | tf_op jit(solution)/shard_map/pallas_call | solution.py:600
  55.5 0.8 %broadcast_in_dim.3 = f32[1,3,32,8]{2,1,3,0:T(4,128)S(1)} reshape(f32[96,8]{0,1:T(8,128)} %bitcast.4) | data formatting | bytes 6144 | tf_op jit(solution)/shard_map/broadcast_in_dim | solution.py:616
  56.3 0.6 %copy.7 = f32[1,3,32,8]{2,3,1,0:T(8,128)} copy(f32[1,3,32,8]{2,1,3,0:T(4,128)S(1)} %broadcast_in_dim.3) | data formatting | bytes 6144
  56.9 2.3 %copy.9 = f32[4,8,32,256]{3,2,1,0:T(8,128)} copy(f32[4,8,32,256]{3,2,1,0:T(8,128)} %get-tuple-element.13) | data formatting | bytes 2097152

commit v3 on v2

--- a/solution.py
+++ b/solution.py
@@ -11,6 +11,7 @@
 from jax.sharding import PartitionSpec as P
 
 LEVELS = 8
+SIDE = 128
 AXES = ("dir", "sy", "sx", "sz", "tile")
 SLAB = AXES[1:4]
 MESH = pl.DeviceIdType.MESH
@@ -45,7 +46,7 @@
     barrier = pltpu.get_barrier_semaphore()
     for peer in peers:
         pl.semaphore_signal(barrier, inc=1, device_id=tuple(peer), device_id_type=MESH)
-    pl.semaphore_wait(barrier, len(peers))
+    return lambda: pl.semaphore_wait(barrier, len(peers))
 
 
 def push(src, dst, send, recv, peer):
@@ -61,7 +62,9 @@
     f32 = jnp.float32
     one = dict(
         grid=(ch, ext, rows, half), wing=(ch, ext, rows, wide),
-        rows=(ch, ext, 8, half), rwing=(ch, ext, 8, wide),
+        rows=(ch, planes, 8, half), rwing=(ch, planes, 8, wide),
+        cut=(2, rows, wide), rcut=(2, rows, wide), brim=(2, ch, half + wide),
+        rbrim=(2, ch, half + wide),
         plane=(2, ch, ext, rows, half), sigma=(2, planes, rows, half),
         slope=(2, planes, rows, half), colour=(2, 3, planes, rows, half),
         through=(2, planes, rows, half), glow=(2, planes, rows, half),
@@ -69,9 +72,11 @@
         codes=(2, rows, half), heading=(2, rows, half), pull=(2, 3, rows, half),
         ahead=(2, planes, rows, half), stack=(lanes, half),
         diff=(2, ch, planes + 4, rows, half), out=(ch, ext, rows, half),
-        line=(ext, ch, half), pack=(rows + 8, max(wide, ch * ext)),
+        line=(ext, ch, half), inpack=(SIDE, SIDE), zpack=(SIDE, SIDE),
+        inturn=(SIDE, SIDE), zturn=(SIDE, SIDE),
         fp=(ch, rows, half), fn=(ch, rows, half),
-        rline=(3, ext, ch, half), rpack=(3, 2, rows + 8, max(wide, ch * ext)),
+        rline=(planes, ch, half), zline=(2, ch, half), rin=(ch * planes, SIDE),
+        rfar=(8, SIDE), rzin=(2, 8, SIDE), rzfar=(2, 8, SIDE),
         tile=(wide, lanes),
         dl=(nz, m, 8, lanes), im=(nz, 2, m, 8, lanes), hd=(nz, m, 8, lanes),
         rdl=(nz, m, 8, lanes), rim=(nz, 2, m, 8, lanes), gm=(ng, m, 8, lanes),
@@ -101,7 +106,50 @@
     return lax.broadcasted_iota(jnp.int32, shape, dim)
 
 
-def sample_plane(b, me, p, keep):
+def lane_of(d, r):
+    return jnp.where(d == 0, r[..., 0:1], r[..., r.shape[-1] - 1:])
+
+
+def inner_edges(b, me, p):
+    rows, wide = b.wing.shape[2:]
+    d, t = me.dir, me.tile
+    fr = lambda r: jnp.where(t == 0, r[0:1], r[7:8])
+
+    def edges(c):
+        edge = jnp.broadcast_to(lane_of(d, b.wing[c, p]), (rows, wide))
+        far = fr(b.rows[c, p - 1])
+        return edge, far, jnp.broadcast_to(lane_of(d, fr(b.rwing[c, p - 1])), (1, wide))
+
+    return edges
+
+
+def outer_edges(b, me, i):
+    rows, wide = b.wing.shape[2:]
+    half = b.grid.shape[3]
+
+    def edges(c):
+        edge = jnp.broadcast_to(b.rcut[i][:, c:c + 1], (rows, wide))
+        line = b.rbrim[i, c:c + 1, :]
+        return edge, line[:, :half], jnp.broadcast_to(lane_of(me.dir, line[:, half:]), (1, wide))
+
+    return edges
+
+
+def cut_faces(b, me):
+    ch, ext, rows, half = b.grid.shape
+    wide = b.wing.shape[3]
+    slot = iota((rows, wide), 1)
+    for i, p in enumerate((ext - 2, 1)):
+        acc = jnp.zeros((rows, wide), jnp.float32)
+        for c in range(ch):
+            acc = jnp.where(slot == c, jnp.broadcast_to(lane_of(me.dir, b.wing[c, p]), (rows, wide)), acc)
+            pick = lambda r: jnp.where(me.tile == 0, r[rows - 1:rows], r[0:1])
+            b.brim[i, c:c + 1, :half] = pick(b.grid[c, p])
+            b.brim[i, c:c + 1, half:] = pick(b.wing[c, p])
+        b.cut[i] = acc
+
+
+def sample_plane(b, me, p, gs, edges, keep):
     ch, _, rows, half = b.grid.shape
     tw = half // 2
     d, t = me.dir, me.tile
@@ -111,12 +159,9 @@
     under = (t == 0).astype(jnp.float32)
     over = 1.0 - under
     for c in range(ch):
-        pick = lambda r: jnp.where(d == 0, r[:, 0:1], r[:, tw - 1:tw])
-        edge = jnp.broadcast_to(pick(b.wing[c, p]), (rows, tw))
-        fr = lambda r: jnp.where(t == 0, r[0:1], r[7:8])
-        ecorner = jnp.broadcast_to(pick(fr(b.rwing[c, p])), (1, tw))
+        edge, line, corner = edges(c)
         m = [b.grid[c, p, :, x * tw:(x + 1) * tw] for x in range(2)] + [edge]
-        far = [fr(b.rows[c, p, :, x * tw:(x + 1) * tw]) for x in range(2)] + [ecorner]
+        far = [line[:, :tw], line[:, tw:], corner]
         up = [jnp.where(row == 0, f * over, pltpu.roll(a, 1, 0)) for a, f in zip(m, far)]
         dn = [jnp.where(row == rows - 1, f * under, pltpu.roll(a, rows - 1, 0))
               for a, f in zip(m, far)]
@@ -130,7 +175,7 @@
             spread.append((lo, a[:2], hi))
         for x in range(2):
             at = slice(x * tw, (x + 1) * tw)
-            for g in range(2):
+            for g in gs:
                 fy, fx = b.pair[g, 1, :, at], b.pair[g, 2, :, at]
                 w00, w01 = b.pair[g, 3, :, at], b.pair[g, 4, :, at]
                 w10, w11 = b.pair[g, 5, :, at], b.pair[g, 6, :, at]
@@ -227,13 +272,12 @@
         lax.fori_loop(0, planes, step, zero)
 
 
-def spill_plane(b, me, p):
+def spill_plane(b, me, p, pack, place):
     ch, ext, rows, half = b.out.shape
     tw = half // 2
     d, t = me.dir, me.tile
     row, lane = iota((rows, tw), 0), iota((rows, tw), 1)
     for c in range(ch):
-        pos = c * ext + p
         cols = []
         for g in range(2):
             fz = b.pair[g, 0]
@@ -262,45 +306,43 @@
         b.out[c, p, :, tw:] = done[1]
         b.line[p, c:c + 1, :tw] = far[0]
         b.line[p, c:c + 1, tw:] = far[1]
-        slot = iota((rows, b.pack.shape[1]), 1)
-        wide = b.pack.shape[1]
-        b.pack[:rows] = jnp.where(
-            slot == pos, jnp.broadcast_to(done[2][:, 0:1], (rows, wide)), b.pack[:rows])
-        b.pack[rows:rows + 1] = jnp.where(
-            slot[0:1] == pos, jnp.broadcast_to(far[2][:, 0:1], (1, wide)), b.pack[rows:rows + 1])
+        slot = iota((rows, SIDE), 1)
+        pos = place(c)
+        pack[:rows] = jnp.where(
+            slot == pos, jnp.broadcast_to(done[2][:, 0:1], (rows, SIDE)), pack[:rows])
+        pack[rows:rows + 1] = jnp.where(
+            slot[0:1] == pos, jnp.broadcast_to(far[2][:, 0:1], (1, SIDE)), pack[rows:rows + 1])
 
 
 def gather_spill(b, me, has_prev, has_next, dest):
     ch, ext, rows, half = b.out.shape
     planes = ext - 2
     tw = half // 2
-    wide = b.pack.shape[1]
     d, t = me.dir, me.tile
     touch = (1 - t) * (rows - 1)
     seam = (1 - d) * (half - 1)
-    slot = iota((rows, wide), 1)
     row = iota((rows, tw), 0)
     lane = iota((rows, tw), 1)
-
-    def merged(i, lo, hi):
-        a = b.rpack[1, i, lo:hi]
-        at = slot[:hi - lo] % ext
-        a = a + jnp.where(at == 1, pltpu.roll(b.rpack[0, i, lo:hi], wide - planes, 1), 0.0) * has_prev
-        return a + jnp.where(at == planes, pltpu.roll(b.rpack[2, i, lo:hi], planes, 1), 0.0) * has_next
-
-    col = merged(0, 0, rows)
-    corner = merged(1, rows, rows + 8)[0:1]
-    col = col + jnp.where(iota((rows, wide), 0) == touch, jnp.broadcast_to(corner, (rows, wide)), 0.0)
+    spot = iota((1, SIDE), 1)
+    b.inturn[:ch * planes] = b.rin[...]
+    for c in range(ch):
+        for k, i, r, has in ((0, 0, ch + c, has_prev), (planes - 1, 1, c, has_next)):
+            far = jnp.broadcast_to(b.rzfar[i, r:r + 1, rows:rows + 1], (1, SIDE))
+            add = jnp.where(spot < rows, b.rzin[i, r:r + 1], 0.0) + jnp.where(spot == touch, far, 0.0)
+            j = c * planes + k
+            b.inturn[j:j + 1] = b.inturn[j:j + 1] + add * has
+    col = b.inturn[...].T[:rows]
+    col = col + jnp.where(iota((rows, SIDE), 0) == touch, jnp.broadcast_to(b.rfar[0:1], (rows, SIDE)), 0.0)
     for c in range(ch):
         for k in range(planes):
-            pos = c * ext + k + 1
-            extra = b.rline[1, k + 1, c:c + 1]
+            pos = c * planes + k
+            extra = b.rline[k, c:c + 1]
             v = b.out[c, k + 1]
             if k == 0:
-                extra = extra + b.rline[0, ext - 1, c:c + 1] * has_prev
+                extra = extra + b.zline[0, c:c + 1] * has_prev
                 v = v + b.fp[c] * has_prev
             if k == planes - 1:
-                extra = extra + b.rline[2, 0, c:c + 1] * has_next
+                extra = extra + b.zline[1, c:c + 1] * has_next
                 v = v + b.fn[c] * has_next
             bar = jnp.broadcast_to(col[:, pos:pos + 1], (rows, tw))
             for x in range(2):
@@ -354,9 +396,16 @@
         across.append(over(p))
         if i:
             gpeer.append(p)
-    greet([prev, nxt] + [flip(p) for p in near] + [over(p) for p in near]
+    ready = greet([prev, nxt] + [flip(p) for p in near] + [over(p) for p in near]
           + [over(flip(p)) for p in near] + zpeer + gpeer + across)
 
+    for c in loads[:2]:
+        c.wait()
+    cut_faces(b, me)
+    for c in loads[2:]:
+        c.wait()
+    weights(b, 0)
+    ready()
     rays = [
         (codes.at[0, :, theirs], b.codes.at[1], mate),
         (head.at[0, :, theirs], b.heading.at[1], mate),
@@ -365,43 +414,41 @@
     rays = [push(x, y, hs.at[i], hr.at[i], p) for i, (x, y, p) in enumerate(rays)]
     for c in rays:
         c.start()
-    for c in loads[:2]:
-        c.wait()
     edge = pl.ds(pl.multiple_of((1 - t) * (rows - 8), 8), 8)
     inner = pl.ds(1, planes)
     beyond = [
-        (b.grid.at[:, inner, edge], b.rows.at[:, inner], flip(me)),
-        (b.wing.at[:, inner, edge], b.rwing.at[:, inner], flip(me)),
+        (b.grid.at[:, inner, edge], b.rows, flip(me)),
+        (b.wing.at[:, inner, edge], b.rwing, flip(me)),
+        (b.cut.at[0], b.rcut.at[0], nxt),
+        (b.cut.at[1], b.rcut.at[1], prev),
+        (b.brim.at[0], b.rbrim.at[0], flip(nxt)),
+        (b.brim.at[1], b.rbrim.at[1], flip(prev)),
         (b.grid.at[:, planes], b.grid.at[:, 0], nxt),
         (b.grid.at[:, 1], b.grid.at[:, ext - 1], prev),
-        (b.wing.at[:, planes], b.wing.at[:, 0], nxt),
-        (b.wing.at[:, 1], b.wing.at[:, ext - 1], prev),
-        (b.grid.at[:, planes, edge], b.rows.at[:, 0], flip(nxt)),
-        (b.grid.at[:, 1, edge], b.rows.at[:, ext - 1], flip(prev)),
-        (b.wing.at[:, planes, edge], b.rwing.at[:, 0], flip(nxt)),
-        (b.wing.at[:, 1, edge], b.rwing.at[:, ext - 1], flip(prev)),
     ]
     beyond = [push(x, y, hs.at[3 + i], hr.at[3 + i], p) for i, (x, y, p) in enumerate(beyond)]
     for c in beyond:
         c.start()
-    for c in loads[2:]:
-        c.wait()
-    weights(b, 0)
+    for c in beyond[:2]:
+        c.wait()
+
+    def inside(gs):
+        def step(p, carry):
+            sample_plane(b, me, p, gs, inner_edges(b, me, p), None)
+            return carry
+
+        lax.fori_loop(1, planes + 1, step, 0)
+
+    inside((0,))
     rays[0].wait()
     weights(b, 1)
-    for c in beyond[:2]:
-        c.wait()
-
-    def inside(p, carry):
-        sample_plane(b, me, p, None)
-        return carry
-
-    lax.fori_loop(1, planes + 1, inside, 0)
+    inside((1,))
     for c in beyond[2:]:
         c.wait()
 
     def ends(i, carry):
-        sample_plane(b, me, i * (ext - 1), jnp.where(i == 0, has_prev, has_next))
+        sample_plane(b, me, i * (ext - 1), (0, 1), outer_edges(b, me, i),
+                     jnp.where(i == 0, has_prev, has_next))
         return carry
 
     lax.fori_loop(0, 2, ends, 0)
@@ -549,20 +596,39 @@
         b.stack[:, x * tw:(x + 1) * tw] = b.tile[...].T
     backward(b, kept)
 
-    def spread(p, carry):
-        spill_plane(b, me, p)
+    def spread_ends(i, carry):
+        spill_plane(b, me, i * (ext - 1), b.zpack, lambda c: i * ch + c)
         return carry
 
-    lax.fori_loop(0, ext, spread, 0)
-    spill = [(b.out.at[:, ext - 1], b.fp, nxt), (b.out.at[:, 0], b.fn, prev)]
-    for i, p in enumerate(near):
-        spill.append((b.line, b.rline.at[2 - i], flip(p)))
-    for i, p in enumerate(near):
-        spill.append((b.pack, b.rpack.at[2 - i, 0], over(p)))
-        spill.append((b.pack, b.rpack.at[2 - i, 1], over(flip(p))))
+    lax.fori_loop(0, 2, spread_ends, 0)
+    b.zturn[...] = b.zpack[...].T
+    spill = [
+        (b.out.at[:, ext - 1], b.fp, nxt), (b.out.at[:, 0], b.fn, prev),
+        (b.line.at[ext - 1], b.zline.at[0], flip(nxt)), (b.line.at[0], b.zline.at[1], flip(prev)),
+    ]
+    small = b.zturn.at[0:8]
+    for i, p in enumerate((nxt, prev)):
+        spill.append((small, b.rzin.at[i], over(p)))
+        spill.append((small, b.rzfar.at[i], over(flip(p))))
     spill = [push(x, y, ss.at[i], sr.at[i], p) for i, (x, y, p) in enumerate(spill)]
     for c in spill:
         c.start()
+
+    def spread(p, carry):
+        spill_plane(b, me, p, b.inpack, lambda c: c * planes + p - 1)
+        return carry
+
+    lax.fori_loop(1, planes + 1, spread, 0)
+    b.inturn[...] = b.inpack[...].T
+    last = [
+        (b.inturn.at[0:ch * planes], b.rin, over(me)),
+        (b.inpack.at[rows:rows + 8], b.rfar, over(flip(me))),
+        (b.line.at[inner], b.rline, flip(me)),
+    ]
+    last = [push(x, y, ss.at[8 + i], sr.at[8 + i], p) for i, (x, y, p) in enumerate(last)]
+    for c in last:
+        c.start()
+    spill = spill + last
 
     for g in range(2):
         for m in range(blocks):
@@ -586,6 +652,12 @@
     for c in spill:
         c.wait()
     gather_spill(b, me, has_prev, has_next, grad)
+
+
+def finish_kernel(rows, src, img, dst, image):
+    dst[...] = src[...]
+    for c in range(3):
+        image[c] = img[:, c * rows:(c + 1) * rows]
 
 
 def per_device(voxels, offsets, heading, cotangent):
@@ -604,7 +676,7 @@
         in_specs=[ANY] * 4,
         out_specs=(VM, VM),
         scratch_shapes=list(room.values()) + [
-            dma(5), dma(13), dma(13),
+            dma(5), dma(11), dma(11),
             dma(nz - 1), dma(nz - 1), dma(nz - 1), dma(nz - 1),
             dma(ng - 1), dma(ng - 1), dma(nz - 1), dma(nz - 1),
             dma(ng), dma(ng), dma(11), dma(11),
@@ -613,7 +685,17 @@
             collective_id=0, has_side_effects=True, vmem_limit_bytes=60 * 1024 * 1024
         ),
     )(voxels, offsets, heading, cotangent)
-    image = img.T.reshape(4, rows, 8)[None, :3]
+    shape = grad.shape
+    block = pl.BlockSpec((1,) + shape[1:], lambda c: (c, 0, 0, 0))
+    grad, image = pl.pallas_call(
+        functools.partial(finish_kernel, rows),
+        grid=(ch,),
+        out_shape=(jax.ShapeDtypeStruct(shape, jnp.float32),
+                   jax.ShapeDtypeStruct((3, 8, rows), jnp.float32)),
+        in_specs=[block, pl.BlockSpec(img.shape, lambda c: (0, 0))],
+        out_specs=(block, pl.BlockSpec((3, 8, rows), lambda c: (0, 0, 0))),
+    )(grad, img)
+    image = jnp.swapaxes(image, 1, 2)[None]
     return (image, grad)
 
 

time: 59.4 us -> 57.9 us (0.975)
  local copies, waits for them, and re-layouts: 3.67 us -> 0 us
  Pallas kernels: 54.9 us -> 57.1 us
    pallas_call x0 -> x1, Pallas kernels: none -> 3.37 us  [per_device(): pl.pallas_call(functools.partial(finish_kernel, rows), grid=(ch,), out_sh...]
    unnamed x2 -> x0, local copies, waits for them, and re-layouts: 2.91 us -> none
    pallas_call x1, Pallas kernels: 54.9 us -> 53.7 us  [per_device(): pl.pallas_call(functools.partial(render_kernel, 2.0 / depth, float(depth)...]
    broadcast_in_dim x1 -> x0, local copies, waits for them, and re-layouts: 0.76 us -> none  [per_device(): image = img.T.reshape(4, rows, 8)[None, :3]]
where the time goes in v3:
time: 57.9 us; the launch traced here: 57.7 us
  Pallas kernels  57.1 us (99%)
  between operations  0.64 us (1%)
    pallas_call x1, Pallas kernels, per_device(): pl.pallas_call(functools.partial(render_kernel, 2.0 / depth, float(depth)...  53.7 us
    pallas_call x1, Pallas kernels, per_device(): pl.pallas_call(functools.partial(finish_kernel, rows), grid=(ch,), out_sh...  3.37 us

profile of v3, /device:TPU:1, one launch (start us, length us, event | category | flops | bytes accessed | tf_op | source)
XLA Modules:
  0.0 57.7 jit_solution(3534603336310152571)
XLA Ops:
  0.6 53.7 %shard_map.59 = (f32[4,8,32,256]{3,2,1,0:T(8,128)}, f32[8,128]{1,0:T(8,128)}) custom-call(f32[4,8,32,512]{3,2,1,0:T(8,128)} %vox.1, s32[1,32,512]{2,1,0:T(8,128)} %codes.1, s32[1,32,512]{2,1,0:T(8,128)} %head.1, f32[1,3,32,512]{3,2,1,0:T(8,128)} %cot.1), custom_call_target="tpu_custom_call" | custom-call | tf_op jit(solution)/shard_map/pallas_call | solution.py:672
  54.4 3.4 %shard_map.60 = (f32[4,8,32,256]{3,2,1,0:T(8,128)}, f32[3,8,32]{2,1,0:T(8,128)}) custom-call(f32[4,8,32,256]{3,2,1,0:T(8,128)} %get-tuple-element.6.src, f32[8,128]{1,0:T(8,128)} %get-tuple-element.7.img), custom_call_target="tpu_custom_call" | custom-call | tf_op jit(solution)/shard_map/pallas_call | solution.py:690

commit v4 on v3

--- a/solution.py
+++ b/solution.py
@@ -15,7 +15,7 @@
 AXES = ("dir", "sy", "sx", "sz", "tile")
 SLAB = AXES[1:4]
 MESH = pl.DeviceIdType.MESH
-ANY = pl.BlockSpec(memory_space=pl.ANY)
+HBM = pl.BlockSpec(memory_space=pltpu.HBM)
 VM = pl.BlockSpec(memory_space=pltpu.VMEM)
 
 
@@ -388,7 +388,8 @@
     for c in loads:
         c.start()
 
-    zpeer = [me._replace(sz=lax.rem(z + i, nz)) for i in range(1, nz)]
+    far_first = sorted(range(1, nz), key=lambda i: -min(i, nz - i))
+    zpeer = [me._replace(sz=lax.rem(z + i, nz)) for i in far_first]
     gpeer, across = [], []
     for i in range(ng):
         g = lax.rem(gi + i, ng)
@@ -648,16 +649,11 @@
     total = b.rpart[0]
     for i in range(1, ng):
         total = total + b.rpart[i]
-    img[...] = total
+    for c in range(3):
+        img[c] = total[:, c * rows:(c + 1) * rows]
     for c in spill:
         c.wait()
     gather_spill(b, me, has_prev, has_next, grad)
-
-
-def finish_kernel(rows, src, img, dst, image):
-    dst[...] = src[...]
-    for c in range(3):
-        image[c] = img[:, c * rows:(c + 1) * rows]
 
 
 def per_device(voxels, offsets, heading, cotangent):
@@ -671,9 +667,9 @@
     dma = lambda n: pltpu.SemaphoreType.DMA((n,))
     grad, img = pl.pallas_call(
         functools.partial(render_kernel, 2.0 / depth, float(depth), tuple(room)),
-        out_shape=(jax.ShapeDtypeStruct((ch, planes, rows, half), jnp.float32),
-                   jax.ShapeDtypeStruct((8, 4 * rows), jnp.float32)),
-        in_specs=[ANY] * 4,
+        out_shape=(pltpu.VMEM((ch, planes, rows, half), jnp.float32),
+                   pltpu.VMEM((3, 8, rows), jnp.float32)),
+        in_specs=[HBM] * 4,
         out_specs=(VM, VM),
         scratch_shapes=list(room.values()) + [
             dma(5), dma(11), dma(11),
@@ -682,20 +678,10 @@
             dma(ng), dma(ng), dma(11), dma(11),
         ],
         compiler_params=pltpu.CompilerParams(
-            collective_id=0, has_side_effects=True, vmem_limit_bytes=60 * 1024 * 1024
+            collective_id=0, has_side_effects=True, vmem_limit_bytes=58 * 1024 * 1024
         ),
     )(voxels, offsets, heading, cotangent)
-    shape = grad.shape
-    block = pl.BlockSpec((1,) + shape[1:], lambda c: (c, 0, 0, 0))
-    grad, image = pl.pallas_call(
-        functools.partial(finish_kernel, rows),
-        grid=(ch,),
-        out_shape=(jax.ShapeDtypeStruct(shape, jnp.float32),
-                   jax.ShapeDtypeStruct((3, 8, rows), jnp.float32)),
-        in_specs=[block, pl.BlockSpec(img.shape, lambda c: (0, 0))],
-        out_specs=(block, pl.BlockSpec((3, 8, rows), lambda c: (0, 0, 0))),
-    )(grad, img)
-    image = jnp.swapaxes(image, 1, 2)[None]
+    image = jnp.swapaxes(img, 1, 2)[None]
     return (image, grad)
 
 

time: 57.9 us -> 53.5 us (0.924)
  Pallas kernels: 57.1 us -> 51.2 us
  local copies, waits for them, and re-layouts: 0 us -> 1.57 us
    pallas_call x1 -> x0, Pallas kernels: 3.37 us -> none  [per_device(): pl.pallas_call(functools.partial(finish_kernel, rows), grid=(ch,), out_sh...]
    pallas_call x1, Pallas kernels: 53.7 us -> 51.2 us  [per_device(): pl.pallas_call(functools.partial(render_kernel, 2.0 / depth, float(depth)...]
    unnamed x0 -> x2, local copies, waits for them, and re-layouts: none -> 1.57 us
where the time goes in v4:
time: 53.5 us; the launch traced here: 53.4 us
  Pallas kernels  51.2 us (96%)
  local copies, waits for them, and re-layouts  1.57 us (3%)
  between operations  0.64 us (1%)
    pallas_call x1, Pallas kernels, per_device(): pl.pallas_call(functools.partial(render_kernel, 2.0 / depth, float(depth)...  51.2 us
    unnamed x2, local copies, waits for them, and re-layouts  1.57 us

profile of v4, /device:TPU:1, one launch (start us, length us, event | category | flops | bytes accessed | tf_op | source)
XLA Modules:
  0.0 53.4 jit_solution(17112641685526756979)
XLA Ops:
  0.6 51.2 %shard_map.59 = (f32[4,8,32,256]{3,2,1,0:T(8,128)S(1)}, f32[3,8,32]{2,1,0:T(8,128)S(1)}) custom-call(f32[4,8,32,512]{3,2,1,0:T(8,128)} %vox.1, s32[1,32,512]{2,1,0:T(8,128)} %codes.1, s32[1,32,512]{2,1,0:T(8,128)} %head.1, f32[1,3,32,512]{3,2,1,0:T(8,128)} %cot.1), custom_call_target="tpu_custom_call" | custom-call | tf_op jit(solution)/shard_map/pallas_call | solution.py:668
  51.9 0.6 %copy.8 = f32[1,3,32,8]{2,3,1,0:T(8,128)} copy(f32[1,3,32,8]{2,3,1,0:T(8,128)S(1)} %bitcast.3) | data formatting | bytes 6144
  52.5 1.0 %copy.9 = f32[4,8,32,256]{3,2,1,0:T(8,128)} copy(f32[4,8,32,256]{3,2,1,0:T(8,128)S(1)} %get-tuple-element.7) | data formatting | bytes 2097152

commit v5 on v4

v5 whole, which is shorter than its diff:
```python
import functools
from types import SimpleNamespace
from typing import NamedTuple

import jax
import jax.numpy as jnp
from jax import lax
from jax.experimental import pallas as pl
from jax.experimental.pallas import tpu as pltpu
from jax.sharding import Mesh
from jax.sharding import PartitionSpec as P

LEVELS = 8
SIDE = 128
AXES = ("dir", "sy", "sx", "sz", "tile")
SLAB = AXES[1:4]
MESH = pl.DeviceIdType.MESH
HBM = pl.BlockSpec(memory_space=pltpu.HBM)
VM = pl.BlockSpec(memory_space=pltpu.VMEM)


class Place(NamedTuple):
    dir: int
    sy: int
    sx: int
    sz: int
    tile: int


def places():
    return Place(*[lax.axis_index(a) for a in AXES])


def slab_index(me):
    _, _, sx, sz, _ = (lax.axis_size(a) for a in AXES)
    return (me.sy * sx + me.sx) * sz + me.sz


def at_slab(me, step):
    sy, sx, sz = (lax.axis_size(a) for a in SLAB)
    s = lax.rem(slab_index(me) + step + sy * sx * sz, sy * sx * sz)
    return me._replace(sy=s // (sx * sz), sx=(s // sz) % sx, sz=s % sz)


def greet(peers):
    barrier = pltpu.get_barrier_semaphore()
    for peer in peers:
        pl.semaphore_signal(barrier, inc=1, device_id=tuple(peer), device_id_type=MESH)
    return lambda: pl.semaphore_wait(barrier, len(peers))


def push(src, dst, send, recv, peer):
    return pltpu.make_async_remote_copy(
        src_ref=src, dst_ref=dst, send_sem=send, recv_sem=recv,
        device_id=tuple(peer), device_id_type=MESH,
    )


def shapes(ch, planes, rows, half, wide, nz, ng):
    lanes, m = 4 * rows, half // 8 // nz
    pairs = m // 2
    ext = planes + 2
    f32 = jnp.float32
    one = dict(
        grid=(ch, ext, rows, half), wing=(ch, ext, rows, wide),
        cut=(2, rows, wide), rcut=(2, rows, wide), brim=(ext, ch, half + wide),
        rbrim=(ext, ch, half + wide),
        plane=(2, ch, ext, rows, half), tail=(2, ext, rows, half),
        sigma=(2, planes, rows, half), colour=(2, 3, planes, rows, half),
        through=(2, planes, rows, half), glow=(2, planes, rows, half),
        taps=(2, 9, rows, half), pair=(2, 7, rows, half), kept=(2, rows, half),
        codes=(2, rows, half), heading=(2, rows, half), pull=(2, 3, rows, half),
        ahead=(2, planes, rows, half), stack=(lanes, wide), tile=(wide, lanes),
        diff=(2, ch + 1, planes + 4, rows, half), out=(ch, ext, rows, half),
        lit=(2, 2, rows, half), seam=(2, 2, rows, SIDE),
        line=(ext, ch, half), pack=(SIDE, SIDE), turn=(SIDE, SIDE),
        fp=(ch, rows, half), fn=(ch, rows, half),
        rline=(planes, ch, half), zline=(2, ch, half), rin=(ch * planes, SIDE),
        rfar=(8, SIDE), rzin=(2, 8, SIDE), rzfar=(2, 8, SIDE),
        dl=(2, nz, pairs, 8, lanes), hd=(2, nz, pairs, 8, lanes), rdl=(2, nz, pairs, 8, lanes),
        im=(2, nz, m, 8, lanes), rim=(2, nz, m, 8, lanes), gm=(2, ng, pairs, 8, lanes),
        zreach=(2, nz, pairs, 8, lanes), zlater=(2, nz, pairs, 8, lanes),
        ret=(2, nz, pairs, 8, lanes), rb=(2, nz, pairs, 8, lanes),
        part=(2, m, 8, lanes), rpart=(ng, 8, lanes),
    )
    ints = dict(codes=0, heading=0)
    return {k: pltpu.VMEM(v, jnp.int32 if k in ints else f32) for k, v in one.items()}


def weights(b, g):
    level = LEVELS
    q = b.codes[g]
    frac = lambda raw: (raw.astype(jnp.float32) + 0.5) / level - 0.5
    fz, fy, fx = frac(q & 7), frac((q >> 3) & 7), frac(q >> 6)
    three = lambda f: (jnp.maximum(-f, 0.0), 1.0 - jnp.abs(f), jnp.maximum(f, 0.0))
    wy, wx = three(fy), three(fx)
    for i in range(3):
        for j in range(3):
            b.taps[g, 3 * i + j] = wy[i] * wx[j]
    ay, ax = jnp.abs(fy), jnp.abs(fx)
    for i, v in enumerate((fz, fy, fx, wy[1] * wx[1], wy[1] * ax, ay * wx[1], ay * ax)):
        b.pair[g, i] = v


def iota(shape, dim):
    return lax.broadcasted_iota(jnp.int32, shape, dim)


def lane_of(d, r):
    return jnp.where(d == 0, r[..., 0:1], r[..., r.shape[-1] - 1:])


def inner_edges(b, me, p):
    return lambda c: jnp.broadcast_to(lane_of(me.dir, b.wing[c, p]), b.wing.shape[2:])


def outer_edges(b, me, i):
    return lambda c: jnp.broadcast_to(b.rcut[i][:, c:c + 1], b.wing.shape[2:])


def cut_faces(b, me):
    ch, ext, rows, half = b.grid.shape
    wide = b.wing.shape[3]
    slot = iota((rows, wide), 1)
    for i, p in enumerate((ext - 2, 1)):
        acc = jnp.zeros((rows, wide), jnp.float32)
        for c in range(ch):
            acc = jnp.where(slot == c, inner_edges(b, me, p)(c), acc)
        b.cut[i] = acc

    def trim(p, carry):
        pick = lambda r: jnp.where(me.tile == 0, r[rows - 1:rows], r[0:1])
        for c in range(ch):
            b.brim[p, c:c + 1, :half] = pick(b.grid[c, p])
            b.brim[p, c:c + 1, half:] = pick(b.wing[c, p])
        return carry

    lax.fori_loop(1, ext - 1, trim, 0)


def sample_plane(b, me, p, gs, edges, keep):
    ch, _, rows, half = b.grid.shape
    tw = half // 2
    d, t = me.dir, me.tile
    row, lane = iota((rows, tw), 0), iota((rows, tw), 1)
    right = (d == 0).astype(jnp.float32)
    left = 1.0 - right
    under = (t == 0).astype(jnp.float32)
    over = 1.0 - under
    for c in range(ch):
        edge, line = edges(c), b.rbrim[p, c:c + 1, :]
        corner = jnp.broadcast_to(lane_of(d, line[:, half:]), (1, tw))
        m = [b.grid[c, p, :, x * tw:(x + 1) * tw] for x in range(2)] + [edge]
        far = [line[:, :tw], line[:, tw:half], corner]
        up = [jnp.where(row == 0, f * over, pltpu.roll(a, 1, 0)) for a, f in zip(m, far)]
        dn = [jnp.where(row == rows - 1, f * under, pltpu.roll(a, rows - 1, 0))
              for a, f in zip(m, far)]
        spread = []
        for a in (up, m, dn):
            r = [pltpu.roll(a[x], 1, 1) for x in range(2)]
            l = [pltpu.roll(a[x], tw - 1, 1) for x in range(2)]
            lo = [jnp.where(lane == 0, a[2] * left, r[0]), jnp.where(lane == 0, r[0], r[1])]
            hi = [jnp.where(lane == tw - 1, l[1], l[0]),
                  jnp.where(lane == tw - 1, a[2] * right, l[1])]
            spread.append((lo, a[:2], hi))
        for x in range(2):
            at = slice(x * tw, (x + 1) * tw)
            for g in gs:
                fy, fx = b.pair[g, 1, :, at], b.pair[g, 2, :, at]
                w00, w01 = b.pair[g, 3, :, at], b.pair[g, 4, :, at]
                w10, w11 = b.pair[g, 5, :, at], b.pair[g, 6, :, at]
                side = lambda s: jnp.where(fx > 0, s[2][x], s[0][x])
                down = fy > 0
                v = (w00 * m[x] + w01 * side(spread[1])
                     + w10 * jnp.where(down, dn[x], up[x])
                     + w11 * jnp.where(down, side(spread[2]), side(spread[0])))
                b.plane[g, c, p, :, at] = v if keep is None else v * keep


def shade_planes(b, scale, g):
    _, ch, ext, rows, half = b.plane.shape
    fz = b.pair[g, 0]
    az = jnp.abs(fz)

    def step(k, acc):
        v = []
        for c in range(ch):
            far = jnp.where(fz > 0, b.plane[g, c, k + 2], b.plane[g, c, k])
            v.append((1.0 - az) * b.plane[g, c, k + 1] + az * far)
        sg = (jnp.maximum(v[0], 0.0) + jnp.log(1.0 + jnp.exp(-jnp.abs(v[0])))) * scale
        b.sigma[g, k] = sg
        b.diff[g, ch, k + 2] = (0.5 + 0.5 * jnp.tanh(0.5 * v[0])) * scale
        for c in range(3):
            b.colour[g, c, k] = 0.5 + 0.5 * jnp.tanh(0.5 * v[c + 1])
        b.ahead[g, k] = acc
        return acc + sg

    return lax.fori_loop(0, ext - 2, step, jnp.zeros((rows, half), jnp.float32))


def local_light(b, total, g):
    _, planes, rows, half = b.sigma.shape
    forward = b.heading[g] == 0

    def step(k, acc):
        sg, ah = b.sigma[g, k], b.ahead[g, k]
        front = jnp.where(forward, ah, total - ah - sg)
        th = jnp.exp(-front)
        gl = th * (1.0 - jnp.exp(-sg))
        b.through[g, k] = th
        b.glow[g, k] = gl
        return tuple(acc[c] + gl * b.colour[g, c, k] for c in range(3))

    zero = jnp.zeros((rows, half), jnp.float32)
    return lax.fori_loop(0, planes, step, (zero,) * 3)


def tiles_out(b, nz, put):
    turned = b.stack[...].T
    for i in range(turned.shape[0] // 8):
        put(i % nz, i // nz, turned[8 * i:8 * i + 8])


def prepare(b, g):
    _, planes, rows, half = b.sigma.shape
    ch = b.grid.shape[0]
    zero = jnp.zeros((rows, half), jnp.float32)
    forward = b.heading[g] == 0
    whole = b.kept[g]
    for c in range(ch + 1):
        for k in (0, 1, planes + 2, planes + 3):
            b.diff[g, c, k] = zero

    def step(k, before):
        pull = [b.pull[g, c] for c in range(3)]
        col = [b.colour[g, c, k] for c in range(3)]
        shade = pull[0] * col[0] + pull[1] * col[1] + pull[2] * col[2]
        th, gl = b.through[g, k], b.glow[g, k]
        share = gl * shade
        later = jnp.where(forward, whole - before - share, before)
        b.diff[g, 0, k + 2] = ((th - gl) * shade - later) * b.diff[g, ch, k + 2]
        for c in range(3):
            b.diff[g, c + 1, k + 2] = pull[c] * gl * (col[c] * (1.0 - col[c]))
        return before + share

    lax.fori_loop(0, planes, step, zero)

    def mix(p, carry):
        fz = b.pair[g, 0]
        mid, up, down = 1.0 - jnp.abs(fz), jnp.maximum(fz, 0.0), jnp.maximum(-fz, 0.0)
        for c in range(ch + 1):
            v = mid * b.diff[g, c, p + 1] + up * b.diff[g, c, p] + down * b.diff[g, c, p + 2]
            if c < ch:
                b.plane[g, c, p] = v
            else:
                b.tail[g, p] = v
        return carry

    lax.fori_loop(0, planes + 2, mix, 0)


def seam_slot(c, p, ch, planes):
    if p == 0:
        return ch * planes + c
    return ch * planes + ch + c if p == planes + 1 else c * planes + p - 1


def seam_of(d, r):
    return jnp.where(d == 0, r[..., r.shape[-1] - 1:], r[..., 0:1])


def gather_seam(b, me, g):
    _, ch, ext, rows, half = b.plane.shape
    slot = iota((rows, SIDE), 1)
    wide = lambda v: jnp.broadcast_to(seam_of(me.dir, v), (rows, SIDE))
    a = jnp.zeros((rows, SIDE), jnp.float32)
    r = a
    for p in range(ext):
        for c in range(ch):
            a = jnp.where(slot == seam_slot(c, p, ch, ext - 2), wide(b.plane[g, c, p]), a)
        r = jnp.where(slot == seam_slot(0, p, ch, ext - 2), wide(b.tail[g, p]), r)
    b.seam[g, 0] = a
    b.seam[g, 1] = r


def spill_seam(b, me):
    _, ch, ext, rows, half = b.plane.shape
    d, t = me.dir, me.tile
    row = iota((rows, SIDE), 0)
    wide = lambda v: jnp.broadcast_to(seam_of(d, v), (rows, SIDE))
    cols = [wide(b.lit[g, 0]) * b.seam[g, 0] - wide(b.lit[g, 1]) * b.seam[g, 1] for g in range(2)]
    bands = []
    for i in range(3):
        w = [jnp.where(d == 0, b.taps[g, 3 * i + 2, :, half - 1:half], b.taps[g, 3 * i, :, 0:1])
             for g in range(2)]
        bands.append(sum(jnp.broadcast_to(w[g], (rows, SIDE)) * cols[g] for g in range(2)))
    up = pltpu.roll(bands[0], rows - 1, 0)
    dn = pltpu.roll(bands[2], 1, 0)
    b.pack[:rows] = (bands[1] + jnp.where(row == rows - 1, 0.0, up) + jnp.where(row == 0, 0.0, dn))
    b.pack[rows:rows + 1] = jnp.where(t == 0, dn[0:1], up[rows - 1:rows])
    b.turn[...] = b.pack[...].T


def spill_plane(b, me, p):
    ch, ext, rows, half = b.out.shape
    tw = half // 2
    t = me.tile
    row, lane = iota((rows, tw), 0), iota((rows, tw), 1)
    for c in range(ch):
        cols = []
        for g in range(2):
            v = b.lit[g, 0] * b.plane[g, c, p]
            cols.append(v if c else v - b.lit[g, 1] * b.tail[g, p])
        bands = []
        for i in range(3):
            u = []
            for j in range(3):
                full = b.taps[0, 3 * i + j] * cols[0] + b.taps[1, 3 * i + j] * cols[1]
                u.append([full[:, :tw], full[:, tw:]])
            l = [pltpu.roll(a, tw - 1, 1) for a in u[0]]
            r = [pltpu.roll(a, 1, 1) for a in u[2]]
            x0 = u[1][0] + jnp.where(lane == tw - 1, l[1], l[0]) + jnp.where(lane == 0, 0.0, r[0])
            x1 = u[1][1] + jnp.where(lane == tw - 1, 0.0, l[1]) + jnp.where(lane == 0, r[0], r[1])
            bands.append([x0, x1])
        for x in range(2):
            at = slice(x * tw, (x + 1) * tw)
            up = pltpu.roll(bands[0][x], rows - 1, 0)
            dn = pltpu.roll(bands[2][x], 1, 0)
            b.out[c, p, :, at] = (bands[1][x] + jnp.where(row == rows - 1, 0.0, up)
                                  + jnp.where(row == 0, 0.0, dn))
            b.line[p, c:c + 1, at] = jnp.where(t == 0, dn[0:1], up[rows - 1:rows])


def gather_spill(b, me, has_prev, has_next, dest):
    ch, ext, rows, half = b.out.shape
    planes = ext - 2
    tw = half // 2
    d, t = me.dir, me.tile
    touch = (1 - t) * (rows - 1)
    seam = (1 - d) * (half - 1)
    row = iota((rows, tw), 0)
    lane = iota((rows, tw), 1)
    spot = iota((1, SIDE), 1)
    b.turn[:ch * planes] = b.rin[...]
    for c in range(ch):
        for k, i, r, has in ((0, 0, ch + c, has_prev), (planes - 1, 1, c, has_next)):
            far = jnp.broadcast_to(b.rzfar[i, r:r + 1, rows:rows + 1], (1, SIDE))
            add = jnp.where(spot < rows, b.rzin[i, r:r + 1], 0.0) + jnp.where(spot == touch, far, 0.0)
            j = c * planes + k
            b.turn[j:j + 1] = b.turn[j:j + 1] + add * has
    col = b.turn[...].T[:rows]
    col = col + jnp.where(iota((rows, SIDE), 0) == touch, jnp.broadcast_to(b.rfar[0:1], (rows, SIDE)), 0.0)
    for c in range(ch):
        for k in range(planes):
            pos = c * planes + k
            extra = b.rline[k, c:c + 1]
            v = b.out[c, k + 1]
            if k == 0:
                extra = extra + b.zline[0, c:c + 1] * has_prev
                v = v + b.fp[c] * has_prev
            if k == planes - 1:
                extra = extra + b.zline[1, c:c + 1] * has_next
                v = v + b.fn[c] * has_next
            bar = jnp.broadcast_to(col[:, pos:pos + 1], (rows, tw))
            for x in range(2):
                at = slice(x * tw, (x + 1) * tw)
                y = v[:, at] + jnp.where(row == touch, jnp.broadcast_to(extra[:, at], (rows, tw)), 0.0)
                y = y + jnp.where(lane + x * tw == seam, bar, 0.0)
                dest[c, k, :, at] = y


def render_kernel(scale, depth, names, vox, codes, head, cot, grad, img, *scratch):
    b = SimpleNamespace(**dict(zip(names, scratch)))
    sems = scratch[len(names):]
    (lsem, hs, hr, s1, r1, s2, r2, s3, r3, s4, r4, s5, r5, ss, sr) = sems
    me = places()
    nsy, nsx, nz = (lax.axis_size(a) for a in SLAB)
    ng = nsy * nsx
    blocks = ng // 2
    d, t, z = me.dir, me.tile, me.sz
    gi = me.sy * nsx + me.sx
    s = slab_index(me)
    prev, nxt = at_slab(me, -1), at_slab(me, 1)
    flip = lambda p: p._replace(tile=1 - p.tile)
    over = lambda p: p._replace(dir=1 - p.dir)
    near = [prev, me, nxt]
    mate = me._replace(dir=1 - d, sx=nsx - 1 - me.sx)
    ch, ext, rows, half = b.grid.shape
    planes = ext - 2
    wide = b.wing.shape[-1]
    has_prev = (s > 0).astype(jnp.float32)
    has_next = (s < nsy * nsx * nz - 1).astype(jnp.float32)

    mine = pl.ds(pl.multiple_of(d * half, half), half)
    theirs = pl.ds(pl.multiple_of((1 - d) * half, half), half)
    beside = pl.ds(pl.multiple_of(half - d * wide, wide), wide)
    loads = [
        (vox.at[:, :, :, mine], b.grid.at[:, 1:planes + 1]),
        (vox.at[:, :, :, beside], b.wing.at[:, 1:planes + 1]),
        (codes.at[0, :, mine], b.codes.at[0]),
        (head.at[0, :, mine], b.heading.at[0]),
        (cot.at[0, :, :, mine], b.pull.at[0]),
    ]
    loads = [pltpu.make_async_copy(a, c, lsem.at[i]) for i, (a, c) in enumerate(loads)]
    for c in loads:
        c.start()

    far_first = sorted(range(1, nz), key=lambda i: -min(i, nz - i))
    zpeer = [me._replace(sz=lax.rem(z + i, nz)) for i in far_first]
    gpeer, across = [], []
    for i in range(ng):
        g = lax.rem(gi + i, ng)
        p = me._replace(sy=g // nsx, sx=g % nsx)
        across.append(over(p))
        if i:
            gpeer.append(p)
    ready = greet([prev, nxt] + [flip(p) for p in near] + [over(prev), over(nxt)]
          + [over(flip(p)) for p in near] + zpeer + gpeer + across)

    for c in loads[:2]:
        c.wait()
    cut_faces(b, me)
    for c in loads[2:]:
        c.wait()
    weights(b, 0)
    ready()
    rays = [
        (codes.at[0, :, theirs], b.codes.at[1], mate),
        (head.at[0, :, theirs], b.heading.at[1], mate),
        (cot.at[0, :, :, theirs], b.pull.at[1], mate),
    ]
    rays = [push(x, y, hs.at[i], hr.at[i], p) for i, (x, y, p) in enumerate(rays)]
    for c in rays:
        c.start()
    inner = pl.ds(1, planes)
    beyond = [
        (b.brim.at[inner], b.rbrim.at[inner], flip(me)),
        (b.cut.at[0], b.rcut.at[0], nxt),
        (b.cut.at[1], b.rcut.at[1], prev),
        (b.brim.at[planes], b.rbrim.at[0], flip(nxt)),
        (b.brim.at[1], b.rbrim.at[ext - 1], flip(prev)),
        (b.grid.at[:, planes], b.grid.at[:, 0], nxt),
        (b.grid.at[:, 1], b.grid.at[:, ext - 1], prev),
    ]
    beyond = [push(x, y, hs.at[3 + i], hr.at[3 + i], p) for i, (x, y, p) in enumerate(beyond)]
    for c in beyond:
        c.start()
    beyond[0].wait()
    tw = half // 2
    pairs = blocks // 2
    first, late = [], []

    def rows_in(parts):
        for n, v in enumerate(parts):
            b.stack[n * rows:(n + 1) * rows] = v

    def chain(g):
        def inside(p, carry):
            sample_plane(b, me, p, (g,), inner_edges(b, me, p), None)
            return carry

        lax.fori_loop(1, planes + 1, inside, 0)
        if g == 0:
            for c in beyond[1:]:
                c.wait()

        def ends(i, carry):
            sample_plane(b, me, i * (ext - 1), (g,), outer_edges(b, me, i),
                         jnp.where(i == 0, has_prev, has_next))
            return carry

        lax.fori_loop(0, 2, ends, 0)
        total = shade_planes(b, scale, g)
        if g == 1:
            for c in rays[1:]:
                c.wait()
        for c in range(3):
            b.pull[g, c] = b.pull[g, c] * depth
        images = local_light(b, total, g)
        kept = sum(b.pull[g, c] * images[c] for c in range(3))
        b.kept[g] = kept
        sides = [slice(0, tw), slice(tw, half)]
        rows_in([v[:, x] for x in sides for v in (total, kept)])

        def put_dl(j, m, v):
            b.dl[g, j, m] = v

        tiles_out(b, nz, put_dl)
        first.append([push(b.dl.at[g, p.sz], b.rdl.at[g, z], s1.at[g * (nz - 1) + i],
                           r1.at[g * (nz - 1) + i], p) for i, p in enumerate(zpeer)])
        for c in first[g]:
            c.start()
        head_f = b.heading[g].astype(jnp.float32)
        rows_in([head_f[:, x] for x in sides for _ in range(2)])

        def put_hd(j, m, v):
            b.hd[g, j, m] = v

        tiles_out(b, nz, put_hd)
        for n, x in enumerate(sides):
            rows_in([v[:, x] for v in images])

            def put_im(j, m, v):
                b.im[g, j, n * pairs + m] = v

            tiles_out(b, nz, put_im)
        late.append([push(b.im.at[g, p.sz], b.rim.at[g, z], s2.at[g * (nz - 1) + i],
                          r2.at[g * (nz - 1) + i], p) for i, p in enumerate(zpeer)])
        for c in late[g]:
            c.start()

    chain(0)
    rays[0].wait()
    weights(b, 1)
    chain(1)
    lanes = b.dl.shape[-1]
    spot = iota(b.dl.shape[2:], 2)
    is_d = (spot // rows) % 2 == 0
    roll = lambda a, n: pltpu.roll(a, n % lanes, 2)

    def directed(parts, ahead):
        lows, low = [], jnp.zeros_like(parts[0])
        for p in parts:
            lows.append(low)
            low = low + p
        highs, high = [], jnp.zeros_like(parts[0])
        for p in reversed(parts):
            highs.append(high)
            high = high + p
        highs = highs[::-1]
        before = [jnp.where(ahead, x, y) for x, y in zip(lows, highs)]
        after = [jnp.where(ahead, y, x) for x, y in zip(lows, highs)]
        return before, after, low

    def compose(g):
        b.rdl[g, z] = b.dl[g, z]
        for c in first[g]:
            c.wait()
        ahead = b.hd[g, z] == 0
        tiles = [b.rdl[g, i] for i in range(nz)]
        before, _, dsum = directed(tiles, ahead)
        reach = [jnp.exp(-x) for x in before]
        _, later, lsum = directed([roll(r, rows) * x for r, x in zip(reach, tiles)], ahead)
        b.gm[g, gi] = jnp.where(is_d, dsum, lsum)
        copies = [push(b.gm.at[g, gi], b.gm.at[g, gi], s3.at[g * (ng - 1) + i],
                       r3.at[g * (ng - 1) + i], p) for i, p in enumerate(gpeer)]
        for c in copies:
            c.start()
        for i in range(nz):
            b.zreach[g, i] = reach[i]
            b.zlater[g, i] = later[i]
        return copies

    def conclude(g, copies):
        for c in copies:
            c.wait()
        ahead = b.hd[g, z] == 0
        groups = [b.gm[g, i] for i in range(ng)]
        before, _, _ = directed(groups, ahead)
        reach = [jnp.exp(-x) for x in before]
        _, after, _ = directed([roll(r, rows) * x for r, x in zip(reach, groups)], ahead)
        to_me = jnp.zeros_like(reach[0])
        rest = jnp.zeros_like(reach[0])
        for i in range(ng):
            to_me = jnp.where(gi == i, reach[i], to_me)
            rest = jnp.where(gi == i, after[i], rest)
        to_me_l = roll(to_me, rows)
        for i in range(nz):
            b.ret[g, i] = jnp.where(is_d, to_me * b.zreach[g, i],
                                    rest + to_me_l * b.zlater[g, i])
        copies = [push(b.ret.at[g, p.sz], b.rb.at[g, z], s4.at[g * (nz - 1) + i],
                       r4.at[g * (nz - 1) + i], p) for i, p in enumerate(zpeer)]
        for c in copies:
            c.start()
        b.rb[g, z] = b.ret[g, z]
        return copies

    second0 = compose(0)
    prepare(b, 0)
    gather_seam(b, me, 0)
    b.rim[0, z] = b.im[0, z]
    second1 = compose(1)
    back0 = conclude(0, second0)
    prepare(b, 1)
    back1 = conclude(1, second1)
    b.rim[1, z] = b.im[1, z]
    gather_seam(b, me, 1)
    for g, back in enumerate((back0, back1)):
        for c in back:
            c.wait()
        for i in range(tw // 8):
            b.tile[8 * i:8 * i + 8] = b.rb[g, i % nz, i // nz]
        turned = b.tile[...].T
        for n in range(4):
            x, q = n // 2, n % 2
            b.lit[g, q, :, x * tw:(x + 1) * tw] = turned[n * rows:(n + 1) * rows]
    def spread_ends(i, carry):
        spill_plane(b, me, i * (ext - 1))
        return carry

    lax.fori_loop(0, 2, spread_ends, 0)
    faces = [
        (b.out.at[:, ext - 1], b.fp, nxt), (b.out.at[:, 0], b.fn, prev),
        (b.line.at[ext - 1], b.zline.at[0], flip(nxt)), (b.line.at[0], b.zline.at[1], flip(prev)),
    ]
    faces = [push(x, y, ss.at[6 + i], sr.at[6 + i], p) for i, (x, y, p) in enumerate(faces)]
    for c in faces:
        c.start()

    spill_seam(b, me)
    small = b.turn.at[ch * planes:ch * planes + 8]
    spill = [
        (b.turn.at[0:ch * planes], b.rin, over(me)),
        (b.pack.at[rows:rows + 8], b.rfar, over(flip(me))),
    ]
    for i, p in enumerate((nxt, prev)):
        spill.append((small, b.rzin.at[i], over(p)))
        spill.append((small, b.rzfar.at[i], over(flip(p))))
    spill = [push(x, y, ss.at[i], sr.at[i], p) for i, (x, y, p) in enumerate(spill)]
    for c in spill:
        c.start()

    for c in late[0] + late[1]:
        c.wait()
    quarter = spot // rows
    for g in range(2):
        for x in range(2):
            total = jnp.zeros(b.dl.shape[2:], jnp.float32)
            for i in range(nz):
                src = b.ret[g, i]
                wash = roll(src, -2 * x * rows)
                wash = jnp.where(quarter == 1, roll(src, (1 - 2 * x) * rows), wash)
                wash = jnp.where(quarter == 2, roll(src, (2 - 2 * x) * rows), wash)
                total = total + wash * b.rim[g, i, x * pairs:(x + 1) * pairs]
            b.part[g, x * pairs:(x + 1) * pairs] = total
    half_of_me = gi // blocks
    out = []
    for g in range(2):
        for m in range(blocks):
            q = blocks * d + m
            peer = me._replace(dir=d if g == 0 else 1 - d, sy=q // nsx, sx=q % nsx)
            out.append(push(b.part.at[g, m], b.rpart.at[gi],
                            s5.at[g * blocks + m], r5.at[gi], peer))
    for g in range(2):
        for m in range(blocks):
            copy = out[g * blocks + m]
            if g == 0:
                itself = gi == blocks * d + m

                @pl.when(itself)
                def _():
                    b.rpart[gi] = b.part[0, m]

                @pl.when(jnp.logical_not(itself))
                def _():
                    copy.start()
            else:
                copy.start()

    def spread(p, carry):
        spill_plane(b, me, p)
        return carry

    lax.fori_loop(1, planes + 1, spread, 0)
    lines = push(b.line.at[inner], b.rline, ss.at[10], sr.at[10], flip(me))
    lines.start()
    spill = spill + faces + [lines]

    for g in range(2):
        for m in range(blocks):
            copy = out[g * blocks + m]
            if g == 0:
                @pl.when(gi != blocks * d + m)
                def _():
                    copy.wait_send()
            else:
                copy.wait_send()
    for i in range(ng):
        arrive = push(b.part.at[0, 0], b.rpart.at[i], s5.at[0], r5.at[i], over(me))

        @pl.when(jnp.logical_or(half_of_me != d, gi != i))
        def _():
            arrive.wait_recv()
    total = b.rpart[0]
    for i in range(1, ng):
        total = total + b.rpart[i]
    for c in range(3):
        img[c] = total[:, c * rows:(c + 1) * rows]
    for c in spill:
        c.wait()
    gather_spill(b, me, has_prev, has_next, grad)


def per_device(voxels, offsets, heading, cotangent):
    ch, planes, rows, total = voxels.shape
    nsy, nsx, nz = (lax.axis_size(a) for a in SLAB)
    ng = nsy * nsx
    depth = planes * nz * ng
    half = total // 2
    wide = half // 2
    room = shapes(ch, planes, rows, half, wide, nz, ng)
    dma = lambda n: pltpu.SemaphoreType.DMA((n,))
    grad, img = pl.pallas_call(
        functools.partial(render_kernel, 2.0 / depth, float(depth), tuple(room)),
        out_shape=(pltpu.VMEM((ch, planes, rows, half), jnp.float32),
                   pltpu.VMEM((3, 8, rows), jnp.float32)),
        in_specs=[HBM] * 4,
        out_specs=(VM, VM),
        scratch_shapes=list(room.values()) + [
            dma(5), dma(10), dma(10),
            dma(2 * nz - 2), dma(2 * nz - 2), dma(2 * nz - 2), dma(2 * nz - 2),
            dma(2 * ng - 2), dma(2 * ng - 2), dma(2 * nz - 2), dma(2 * nz - 2),
            dma(ng), dma(ng), dma(11), dma(11),
        ],
        compiler_params=pltpu.CompilerParams(
            collective_id=0, has_side_effects=True, vmem_limit_bytes=58 * 1024 * 1024
        ),
    )(voxels, offsets, heading, cotangent)
    image = jnp.swapaxes(img, 1, 2)[None]
    return (image, grad)


def solution(mesh):
    n = mesh.devices.size
    shape = (2, 4, 2, 8, 2) if n == 256 else (2,) * 5
    finer = Mesh(mesh.devices.reshape(shape), AXES)
    return jax.shard_map(
        per_device,
        mesh=finer,
        in_specs=(
            P(None, SLAB, "tile", None),
            P("dir", "tile", None),
            P("dir", "tile", None),
            P("dir", None, "tile", None),
        ),
        out_specs=(P("dir", None, "tile", SLAB), P(None, SLAB, "tile", "dir")),
        check_vma=False,
    )
```

time: 53.5 us -> 50.7 us (0.948)
  Pallas kernels: 51.2 us -> 48.4 us
    pallas_call x1, Pallas kernels: 51.2 us -> 48.4 us  [per_device(): pl.pallas_call(functools.partial(render_kernel, 2.0 / depth, float(depth)...]
where the time goes in v5:
time: 50.7 us; the launch traced here: 50.6 us
  Pallas kernels  48.4 us (95%)
  local copies, waits for them, and re-layouts  1.57 us (3%)
  between operations  0.64 us (1%)
    pallas_call x1, Pallas kernels, per_device(): pl.pallas_call(functools.partial(render_kernel, 2.0 / depth, float(depth)...  48.4 us
    unnamed x2, local copies, waits for them, and re-layouts  1.57 us

profile of v5, /device:TPU:1, one launch (start us, length us, event | category | flops | bytes accessed | tf_op | source)
XLA Modules:
  0.0 50.6 jit_solution(12388788101434973292)
XLA Ops:
  0.6 48.4 %shard_map.59 = (f32[4,8,32,256]{3,2,1,0:T(8,128)S(1)}, f32[3,8,32]{2,1,0:T(8,128)S(1)}) custom-call(f32[4,8,32,512]{3,2,1,0:T(8,128)} %vox.1, s32[1,32,512]{2,1,0:T(8,128)} %codes.1, s32[1,32,512]{2,1,0:T(8,128)} %head.1, f32[1,3,32,512]{3,2,1,0:T(8,128)} %cot.1), custom_call_target="tpu_custom_call" | custom-call | tf_op jit(solution)/shard_map/pallas_call | solution.py:703
  49.0 0.6 %copy.8 = f32[1,3,32,8]{2,3,1,0:T(8,128)} copy(f32[1,3,32,8]{2,3,1,0:T(8,128)S(1)} %bitcast.3) | data formatting | bytes 6144
  49.6 1.0 %copy.9 = f32[4,8,32,256]{3,2,1,0:T(8,128)} copy(f32[4,8,32,256]{3,2,1,0:T(8,128)S(1)} %get-tuple-element.7) | data formatting | bytes 2097152

commit v6 on v5

--- a/solution.py
+++ b/solution.py
@@ -65,6 +65,7 @@
         grid=(ch, ext, rows, half), wing=(ch, ext, rows, wide),
         cut=(2, rows, wide), rcut=(2, rows, wide), brim=(ext, ch, half + wide),
         rbrim=(ext, ch, half + wide),
+        shift=(8, ch, ext, rows, half),
         plane=(2, ch, ext, rows, half), tail=(2, ext, rows, half),
         sigma=(2, planes, rows, half), colour=(2, 3, planes, rows, half),
         through=(2, planes, rows, half), glow=(2, planes, rows, half),
@@ -163,6 +164,9 @@
             hi = [jnp.where(lane == tw - 1, l[1], l[0]),
                   jnp.where(lane == tw - 1, a[2] * right, l[1])]
             spread.append((lo, a[:2], hi))
+        for n, v in enumerate([up, dn] + [q[0] for q in spread] + [q[2] for q in spread]):
+            b.shift[n, c, p, :, :tw] = v[0]
+            b.shift[n, c, p, :, tw:] = v[1]
         for x in range(2):
             at = slice(x * tw, (x + 1) * tw)
             for g in gs:
@@ -175,6 +179,17 @@
                      + w10 * jnp.where(down, dn[x], up[x])
                      + w11 * jnp.where(down, side(spread[2]), side(spread[0])))
                 b.plane[g, c, p, :, at] = v if keep is None else v * keep
+
+
+def sample_again(b, p, g, keep):
+    right, down = b.pair[g, 2] > 0, b.pair[g, 1] > 0
+    for c in range(b.grid.shape[0]):
+        up, dn, *sides = [b.shift[n, c, p] for n in range(8)]
+        side = [jnp.where(right, sides[n + 3], sides[n]) for n in range(3)]
+        v = (b.pair[g, 3] * b.grid[c, p] + b.pair[g, 4] * side[1]
+             + b.pair[g, 5] * jnp.where(down, dn, up)
+             + b.pair[g, 6] * jnp.where(down, side[2], side[0]))
+        b.plane[g, c, p] = v if keep is None else v * keep
 
 
 def shade_planes(b, scale, g):
@@ -456,7 +471,10 @@
 
     def chain(g):
         def inside(p, carry):
-            sample_plane(b, me, p, (g,), inner_edges(b, me, p), None)
+            if g == 0:
+                sample_plane(b, me, p, (g,), inner_edges(b, me, p), None)
+            else:
+                sample_again(b, p, g, None)
             return carry
 
         lax.fori_loop(1, planes + 1, inside, 0)
@@ -465,8 +483,11 @@
                 c.wait()
 
         def ends(i, carry):
-            sample_plane(b, me, i * (ext - 1), (g,), outer_edges(b, me, i),
-                         jnp.where(i == 0, has_prev, has_next))
+            keep = jnp.where(i == 0, has_prev, has_next)
+            if g == 0:
+                sample_plane(b, me, i * (ext - 1), (g,), outer_edges(b, me, i), keep)
+            else:
+                sample_again(b, i * (ext - 1), g, keep)
             return carry
 
         lax.fori_loop(0, 2, ends, 0)
@@ -506,8 +527,9 @@
             tiles_out(b, nz, put_im)
         late.append([push(b.im.at[g, p.sz], b.rim.at[g, z], s2.at[g * (nz - 1) + i],
                           r2.at[g * (nz - 1) + i], p) for i, p in enumerate(zpeer)])
-        for c in late[g]:
-            c.start()
+        if g == 0:
+            for c in late[g]:
+                c.start()
 
     chain(0)
     rays[0].wait()
@@ -583,6 +605,8 @@
     back0 = conclude(0, second0)
     prepare(b, 1)
     back1 = conclude(1, second1)
+    for c in late[1]:
+        c.start()
     b.rim[1, z] = b.im[1, z]
     gather_seam(b, me, 1)
     for g, back in enumerate((back0, back1)):
@@ -594,19 +618,13 @@
         for n in range(4):
             x, q = n // 2, n % 2
             b.lit[g, q, :, x * tw:(x + 1) * tw] = turned[n * rows:(n + 1) * rows]
-    def spread_ends(i, carry):
-        spill_plane(b, me, i * (ext - 1))
-        return carry
-
-    lax.fori_loop(0, 2, spread_ends, 0)
-    faces = [
-        (b.out.at[:, ext - 1], b.fp, nxt), (b.out.at[:, 0], b.fn, prev),
-        (b.line.at[ext - 1], b.zline.at[0], flip(nxt)), (b.line.at[0], b.zline.at[1], flip(prev)),
-    ]
-    faces = [push(x, y, ss.at[6 + i], sr.at[6 + i], p) for i, (x, y, p) in enumerate(faces)]
-    for c in faces:
-        c.start()
-
+    faces = []
+    for i, (p, to, r, zl) in enumerate(((ext - 1, nxt, b.fp, 0), (0, prev, b.fn, 1))):
+        spill_plane(b, me, p)
+        faces += [push(b.out.at[:, p], r, ss.at[6 + 2 * i], sr.at[6 + 2 * i], to),
+                  push(b.line.at[p], b.zline.at[zl], ss.at[7 + 2 * i], sr.at[7 + 2 * i], flip(to))]
+        for c in faces[2 * i:]:
+            c.start()
     spill_seam(b, me)
     small = b.turn.at[ch * planes:ch * planes + 8]
     spill = [

time: 50.7 us -> 47.9 us (0.945)
  Pallas kernels: 48.4 us -> 45.6 us
    pallas_call x1, Pallas kernels: 48.4 us -> 45.6 us  [per_device(): pl.pallas_call(functools.partial(render_kernel, 2.0 / depth, float(depth)...]
where the time goes in v6:
time: 47.9 us; the launch traced here: 47.8 us
  Pallas kernels  45.6 us (95%)
  local copies, waits for them, and re-layouts  1.57 us (3%)
  between operations  0.64 us (1%)
    pallas_call x1, Pallas kernels, per_device(): pl.pallas_call(functools.partial(render_kernel, 2.0 / depth, float(depth)...  45.6 us
    unnamed x2, local copies, waits for them, and re-layouts  1.57 us

profile of v6, /device:TPU:1, one launch (start us, length us, event | category | flops | bytes accessed | tf_op | source)
XLA Modules:
  0.0 47.8 jit_solution(1002299576840524574)
XLA Ops:
  0.6 45.6 %shard_map.59 = (f32[4,8,32,256]{3,2,1,0:T(8,128)S(1)}, f32[3,8,32]{2,1,0:T(8,128)S(1)}) custom-call(f32[4,8,32,512]{3,2,1,0:T(8,128)} %vox.1, s32[1,32,512]{2,1,0:T(8,128)} %codes.1, s32[1,32,512]{2,1,0:T(8,128)} %head.1, f32[1,3,32,512]{3,2,1,0:T(8,128)} %cot.1), custom_call_target="tpu_custom_call" | custom-call | tf_op jit(solution)/shard_map/pallas_call | solution.py:721
  46.2 0.6 %copy.8 = f32[1,3,32,8]{2,3,1,0:T(8,128)} copy(f32[1,3,32,8]{2,3,1,0:T(8,128)S(1)} %bitcast.3) | data formatting | bytes 6144
  46.8 1.0 %copy.9 = f32[4,8,32,256]{3,2,1,0:T(8,128)} copy(f32[4,8,32,256]{3,2,1,0:T(8,128)S(1)} %get-tuple-element.7) | data formatting | bytes 2097152

commit v7 on v6

--- a/solution.py
+++ b/solution.py
@@ -372,10 +372,8 @@
             v = b.out[c, k + 1]
             if k == 0:
                 extra = extra + b.zline[0, c:c + 1] * has_prev
-                v = v + b.fp[c] * has_prev
             if k == planes - 1:
                 extra = extra + b.zline[1, c:c + 1] * has_next
-                v = v + b.fn[c] * has_next
             bar = jnp.broadcast_to(col[:, pos:pos + 1], (rows, tw))
             for x in range(2):
                 at = slice(x * tw, (x + 1) * tw)
@@ -478,7 +476,15 @@
             return carry
 
         lax.fori_loop(1, planes + 1, inside, 0)
+        sides = [slice(0, tw), slice(tw, half)]
         if g == 0:
+            head_f = b.heading[g].astype(jnp.float32)
+            rows_in([head_f[:, x] for x in sides for _ in range(2)])
+
+            def put_hd(j, m, v):
+                b.hd[g, j, m] = v
+
+            tiles_out(b, nz, put_hd)
             for c in beyond[1:]:
                 c.wait()
 
@@ -511,13 +517,14 @@
                            r1.at[g * (nz - 1) + i], p) for i, p in enumerate(zpeer)])
         for c in first[g]:
             c.start()
-        head_f = b.heading[g].astype(jnp.float32)
-        rows_in([head_f[:, x] for x in sides for _ in range(2)])
-
-        def put_hd(j, m, v):
-            b.hd[g, j, m] = v
-
-        tiles_out(b, nz, put_hd)
+        if g == 1:
+            head_f = b.heading[g].astype(jnp.float32)
+            rows_in([head_f[:, x] for x in sides for _ in range(2)])
+
+            def put_hd(j, m, v):
+                b.hd[g, j, m] = v
+
+            tiles_out(b, nz, put_hd)
         for n, x in enumerate(sides):
             rows_in([v[:, x] for v in images])
 
@@ -602,11 +609,11 @@
     gather_seam(b, me, 0)
     b.rim[0, z] = b.im[0, z]
     second1 = compose(1)
+    for c in late[1]:
+        c.start()
     back0 = conclude(0, second0)
     prepare(b, 1)
     back1 = conclude(1, second1)
-    for c in late[1]:
-        c.start()
     b.rim[1, z] = b.im[1, z]
     gather_seam(b, me, 1)
     for g, back in enumerate((back0, back1)):
@@ -682,7 +689,7 @@
     lax.fori_loop(1, planes + 1, spread, 0)
     lines = push(b.line.at[inner], b.rline, ss.at[10], sr.at[10], flip(me))
     lines.start()
-    spill = spill + faces + [lines]
+    spill = spill + [faces[1], faces[3], lines]
 
     for g in range(2):
         for m in range(blocks):
@@ -707,6 +714,11 @@
     for c in spill:
         c.wait()
     gather_spill(b, me, has_prev, has_next, grad)
+    for c in (faces[0], faces[2]):
+        c.wait()
+    for c in range(ch):
+        grad[c, 0] = grad[c, 0] + b.fp[c] * has_prev
+        grad[c, planes - 1] = grad[c, planes - 1] + b.fn[c] * has_next
 
 
 def per_device(voxels, offsets, heading, cotangent):

time: 47.9 us -> 48 us (level)
  no operation moved by 1% of the time
where the time goes in v7:
time: 48 us; the launch traced here: 47.9 us
  Pallas kernels  45.7 us (95%)
  local copies, waits for them, and re-layouts  1.57 us (3%)
  between operations  0.64 us (1%)
    pallas_call x1, Pallas kernels, per_device(): pl.pallas_call(functools.partial(render_kernel, 2.0 / depth, float(depth)...  45.7 us
    unnamed x2, local copies, waits for them, and re-layouts  1.57 us

profile of v7, /device:TPU:1, one launch (start us, length us, event | category | flops | bytes accessed | tf_op | source)
XLA Modules:
  0.0 47.9 jit_solution(6898976075495593265)
XLA Ops:
  0.6 45.7 %shard_map.59 = (f32[4,8,32,256]{3,2,1,0:T(8,128)S(1)}, f32[3,8,32]{2,1,0:T(8,128)S(1)}) custom-call(f32[4,8,32,512]{3,2,1,0:T(8,128)} %vox.1, s32[1,32,512]{2,1,0:T(8,128)} %codes.1, s32[1,32,512]{2,1,0:T(8,128)} %head.1, f32[1,3,32,512]{3,2,1,0:T(8,128)} %cot.1), custom_call_target="tpu_custom_call" | custom-call | tf_op jit(solution)/shard_map/pallas_call | solution.py:733
  46.4 0.6 %copy.8 = f32[1,3,32,8]{2,3,1,0:T(8,128)} copy(f32[1,3,32,8]{2,3,1,0:T(8,128)S(1)} %bitcast.3) | data formatting | bytes 6144
  47.0 1.0 %copy.9 = f32[4,8,32,256]{3,2,1,0:T(8,128)} copy(f32[4,8,32,256]{3,2,1,0:T(8,128)S(1)} %get-tuple-element.7) | data formatting | bytes 2097152
